TPU v7x, 32 devices: a whole 2x2x4 slice. The times are simulated.
32 devices in a mesh: gx: 8 (over z, x), yz: 4 (over y, core).
Axes of the slice: x: 2, y: 2, z: 4, core: 2. Of those that a mesh axis runs over, the one named last changes fastest.
Arguments:
- state: float32 [4, 256, 192, 256], P(None, 'gx', 'yz'), may hold values from -6 to 6
- mean_flow: float32 [256, 192, 256], P('gx', 'yz'), may hold values from 0.2 to 1.2
- face_cell: int32 [6144], P(('gx', 'yz')), may hold values from 0 to 12582911, as said below
- face_normal: float32 [3, 6144], P(None, ('gx', 'yz')), may hold values from -3 to 3
- face_pos: float32 [3, 6144], P(None, ('gx', 'yz')), may hold values from -2 to 2
- observer_pos: float32 [3, 512], replicated, may hold values from 4 to 12
- time_bin: int32 [6144, 512], P(('gx', 'yz')), may hold values from 0 to 63
Outputs:
- state_next: float32 [4, 256, 192, 256], P(None, 'gx', 'yz')
- signal: float32 [512, 64], P(('gx', 'yz'))
Inputs may be any that keep to these rules, and one draw needn't show every extreme that they name: `face_cell`: face j is held by device j // 192 of gx+yz, and its cell, numbered (x 192 + y) * 256 + z, lies in that device's block of grid cells.
All inputs are finite; a program needn't handle non-finite values.
Results may differ from a plain program's by a relative error of at most 0.000084.
Values sent between devices are 32-bit elements; how exact they have to be, the bound alone decides.
A program may use at most 192 MiB of HBM per device.

v0:
```python
import jax
import jax.numpy as jnp
from jax import lax
from jax.sharding import PartitionSpec as P

BINS = 64


time_step = 0.25
four_pi = 4.0 * 3.141592653589793
highest = lax.Precision.HIGHEST


def extended(block, sides, width):
    for axis, dim in sides:
        count = lax.axis_size(axis)
        forward = [(i, i + 1) for i in range(count - 1)]
        backward = [(target, source) for source, target in forward]
        low = lax.ppermute(
            lax.slice_in_dim(block, block.shape[dim] - width, None, axis=dim), axis, forward
        )
        high = lax.ppermute(lax.slice_in_dim(block, 0, width, axis=dim), axis, backward)
        block = jnp.concatenate([low, block, high], axis=dim)
    return block


def diagonals(count):
    index = jnp.arange(count)
    third = jnp.full((count,), 1.0 / 3.0, jnp.float32)
    quarter = jnp.float32(0.25)
    lower = jnp.where(index == 1, quarter, third)
    lower = jnp.where(index == count - 2, quarter, lower)
    lower = jnp.where(index == count - 1, jnp.float32(2.0), lower)
    lower = jnp.where(index == 0, jnp.float32(0.0), lower)
    upper = jnp.where(index == 1, quarter, third)
    upper = jnp.where(index == count - 2, quarter, upper)
    upper = jnp.where(index == 0, jnp.float32(2.0), upper)
    upper = jnp.where(index == count - 1, jnp.float32(0.0), upper)
    return (lower, jnp.ones((count,), jnp.float32), upper)


def inverse_of(lower, middle, upper):
    count = middle.shape[0]
    return lax.linalg.tridiagonal_solve(lower, middle, upper, jnp.eye(count, dtype=jnp.float32))


def compact_rhs(field, axis):
    count = field.shape[axis]
    widths = [(2, 2) if dimension == axis else (0, 0) for dimension in range(field.ndim)]
    padded = jnp.pad(field, widths)

    def take(first, last):
        return lax.slice_in_dim(padded, first, last, axis=axis)

    def plane(index):
        return lax.slice_in_dim(field, index, index + 1, axis=axis)

    inner = 7.0 / 9.0 * (take(3, count + 3) - take(1, count + 1)) + 1.0 / 36.0 * (
        take(4, count + 4) - take(0, count)
    )
    first_row = 0.5 * (4.0 * plane(1) + plane(2) - 5.0 * plane(0))
    second_row = 0.75 * (plane(2) - plane(0))
    before_last = 0.75 * (plane(count - 1) - plane(count - 3))
    last_row = 0.5 * (5.0 * plane(count - 1) - 4.0 * plane(count - 2) - plane(count - 3))
    middle_rows = lax.slice_in_dim(inner, 2, count - 2, axis=axis)
    return jnp.concatenate([first_row, second_row, middle_rows, before_last, last_row], axis)


def explicit_y(padded, count):

    def take(shift):
        return lax.slice_in_dim(padded, 3 + shift, 3 + shift + count, axis=2)

    return (
        0.75 * (take(1) - take(-1))
        - 0.15 * (take(2) - take(-2))
        + 1.0 / 60.0 * (take(3) - take(-3))
    )


def transposed_x(fields):
    part = lax.all_to_all(fields, "gx", split_axis=2, concat_axis=1, tiled=True)
    inverse = inverse_of(*diagonals(part.shape[1]))
    rhs = compact_rhs(part, 1)
    solved = jnp.einsum("ij,fjab->fiab", inverse, rhs, precision=highest)
    return lax.all_to_all(solved, "gx", split_axis=1, concat_axis=2, tiled=True)


def per_device(state, mean_flow, face_cell, face_normal, face_pos, observer_pos, time_bin):
    cells, width, depth = (state.shape[1], state.shape[2], state.shape[3])
    fields = jnp.concatenate([state, mean_flow[None]], 0)
    x_rates = transposed_x(fields)
    crossing = extended(fields[0::2], (("yz", 2),), 3)
    y_rates = explicit_y(crossing, width)
    z_fields = jnp.concatenate([fields[0:1], fields[3:5]], 0)
    z_inverse = inverse_of(*diagonals(depth))
    z_rates = jnp.dot(compact_rhs(z_fields, 3), z_inverse.T, precision=highest)
    pressure, stream, lateral, vertical = (state[0], state[1], state[2], state[3])
    pressure_rate = -(mean_flow * x_rates[0] + x_rates[1] + y_rates[1] + z_rates[1])
    stream_rate = -(
        mean_flow * x_rates[1]
        + stream * x_rates[4]
        + lateral * y_rates[2]
        + vertical * z_rates[2]
        + x_rates[0]
    )
    lateral_rate = -(mean_flow * x_rates[2] + y_rates[0])
    vertical_rate = -(mean_flow * x_rates[3] + z_rates[0])
    rates = jnp.stack([pressure_rate, stream_rate, lateral_rate, vertical_rate])
    state_next = state + time_step * rates
    planes = width * lax.axis_size("yz")
    block = lax.axis_index("gx")
    group = lax.axis_index("yz")
    along_x = face_cell // (planes * depth) - block * cells
    along_y = face_cell // depth % planes - group * width
    along_z = face_cell % depth
    local_cell = (along_x * width + along_y) * depth + along_z
    face_rates = rates.reshape(4, -1)[:, local_cell]
    face_pressure = state_next[0].reshape(-1)[local_cell]
    normal_rate = (
        face_normal[0] * face_rates[1]
        + face_normal[1] * face_rates[2]
        + face_normal[2] * face_rates[3]
    )
    offset_x = observer_pos[0][None, :] - face_pos[0][:, None]
    offset_y = observer_pos[1][None, :] - face_pos[1][:, None]
    offset_z = observer_pos[2][None, :] - face_pos[2][:, None]
    distance = jnp.sqrt(offset_x * offset_x + offset_y * offset_y + offset_z * offset_z)
    normal_r = (
        face_normal[0][:, None] * offset_x
        + face_normal[1][:, None] * offset_y
        + face_normal[2][:, None] * offset_z
    ) / distance
    contribution = (
        normal_rate[:, None]
        + (face_rates[0][:, None] + face_pressure[:, None] / distance) * normal_r
    ) / (four_pi * distance)
    onehot = (time_bin[:, :, None] == jnp.arange(BINS, dtype=jnp.int32)).astype(jnp.float32)
    signal = lax.psum_scatter(
        jnp.sum(contribution[:, :, None] * onehot, axis=0),
        ("gx", "yz"),
        scatter_dimension=0,
        tiled=True,
    )
    return (state_next, signal)


def solution(mesh):
    in_specs = (
        P(None, "gx", "yz", None),
        P("gx", "yz", None),
        P(("gx", "yz")),
        P(None, ("gx", "yz")),
        P(None, ("gx", "yz")),
        P(),
        P(("gx", "yz"), None),
    )
    out_specs = (P(None, "gx", "yz", None), P(("gx", "yz"), None))
    return jax.shard_map(
        per_device, mesh=mesh, in_specs=in_specs, out_specs=out_specs, check_vma=False
    )
```

profile of v0, /device:TPU:0, one launch (start us, length us, event | category | flops | bytes accessed | tf_op | source)
XLA Modules:
  0.0 1276.5 jit_solution(14212559706522243462)
XLA Ops:
  31.2 458.7 %while.8 = (s32[]{:T(128)}, f32[]{:T(128)}, f32[256]{0:T(256)S(1)}, f32[7,32]{1,0:T(8,128)S(1)}, f32[7,32,256]{2,1,0:T(8,128)S(1)}, /*index=5*/f32[7,32]{1,0:T(8...) while((s32[]{:T(128)}, f32[]{:T(128)}, ...), condition=%wide.region_1.2_spmd, body=%wide.region_0.1_spmd.sunk | while | flops 24705 | bytes 269033 | solution.py:44
  74.5 20.3 %subtract_divide_fusion.125 = (f32[256]{0:T(256)S(1)}, f32[256]{0:T(256)S(1)}, f32[256]{0:T(256)S(1)}, f32[256]{0:T(256)S(1)}, f32[256]{0:T(256)S(1)}, /*index=5...) fusion(f32[256]{0:T(256)S(1)} %bitcast.1217, ...), kind=kLoop, calls=%fused_computation.37.clone.1 | loop fusion | flops 24576 | bytes 66816 | tf_op jit(solution)/shard_map/while/body/eval_jaxpr/div | solution.py:44
  140.0 20.3 %subtract_divide_fusion.125 = (f32[256]{0:T(256)S(1)}, f32[256]{0:T(256)S(1)}, f32[256]{0:T(256)S(1)}, f32[256]{0:T(256)S(1)}, f32[256]{0:T(256)S(1)}, /*index=5...) fusion(f32[256]{0:T(256)S(1)} %bitcast.1217, ...), kind=kLoop, calls=%fused_computation.37.clone.1 | loop fusion | flops 24576 | bytes 66816 | tf_op jit(solution)/shard_map/while/body/eval_jaxpr/div | solution.py:44
  205.5 20.3 %subtract_divide_fusion.125 = (f32[256]{0:T(256)S(1)}, f32[256]{0:T(256)S(1)}, f32[256]{0:T(256)S(1)}, f32[256]{0:T(256)S(1)}, f32[256]{0:T(256)S(1)}, /*index=5...) fusion(f32[256]{0:T(256)S(1)} %bitcast.1217, ...), kind=kLoop, calls=%fused_computation.37.clone.1 | loop fusion | flops 24576 | bytes 66816 | tf_op jit(solution)/shard_map/while/body/eval_jaxpr/div | solution.py:44
  271.0 20.3 %subtract_divide_fusion.125 = (f32[256]{0:T(256)S(1)}, f32[256]{0:T(256)S(1)}, f32[256]{0:T(256)S(1)}, f32[256]{0:T(256)S(1)}, f32[256]{0:T(256)S(1)}, /*index=5...) fusion(f32[256]{0:T(256)S(1)} %bitcast.1217, ...), kind=kLoop, calls=%fused_computation.37.clone.1 | loop fusion | flops 24576 | bytes 66816 | tf_op jit(solution)/shard_map/while/body/eval_jaxpr/div | solution.py:44
  336.6 20.3 %subtract_divide_fusion.125 = (f32[256]{0:T(256)S(1)}, f32[256]{0:T(256)S(1)}, f32[256]{0:T(256)S(1)}, f32[256]{0:T(256)S(1)}, f32[256]{0:T(256)S(1)}, /*index=5...) fusion(f32[256]{0:T(256)S(1)} %bitcast.1217, ...), kind=kLoop, calls=%fused_computation.37.clone.1 | loop fusion | flops 24576 | bytes 66816 | tf_op jit(solution)/shard_map/while/body/eval_jaxpr/div | solution.py:44
  402.1 20.3 %subtract_divide_fusion.125 = (f32[256]{0:T(256)S(1)}, f32[256]{0:T(256)S(1)}, f32[256]{0:T(256)S(1)}, f32[256]{0:T(256)S(1)}, f32[256]{0:T(256)S(1)}, /*index=5...) fusion(f32[256]{0:T(256)S(1)} %bitcast.1217, ...), kind=kLoop, calls=%fused_computation.37.clone.1 | loop fusion | flops 24576 | bytes 66816 | tf_op jit(solution)/shard_map/while/body/eval_jaxpr/div | solution.py:44
  467.6 20.3 %subtract_divide_fusion.125 = (f32[256]{0:T(256)S(1)}, f32[256]{0:T(256)S(1)}, f32[256]{0:T(256)S(1)}, f32[256]{0:T(256)S(1)}, f32[256]{0:T(256)S(1)}, /*index=5...) fusion(f32[256]{0:T(256)S(1)} %bitcast.1217, ...), kind=kLoop, calls=%fused_computation.37.clone.1 | loop fusion | flops 24576 | bytes 66816 | tf_op jit(solution)/shard_map/while/body/eval_jaxpr/div | solution.py:44
  529.7 19.0 %subtract_divide_fusion.32 = (f32[256]{0:T(256)S(1)}, f32[256]{0:T(256)S(1)}, f32[256]{0:T(256)S(1)}, f32[256]{0:T(256)S(1)}, f32[256]{0:T(256)S(1)}, /*index=5*...) fusion(f32[256]{0:T(256)S(1)} %bitcast.1418, ...), kind=kLoop, calls=%fused_computation.305 | loop fusion | flops 23808 | bytes 64760 | tf_op jit(solution)/shard_map/eval_jaxpr/div | solution.py:44
  551.3 151.0 %while.9 = (s32[]{:T(128)}, f32[256]{0:T(256)S(1)}, f32[7,32,256]{2,1,0:T(8,128)S(1)}, f32[7,32,256]{2,1,0:T(8,128)S(1)}, f32[7,32]{1,0:T(8,128)S(1)}, /*index=5...) while((s32[]{:T(128)}, f32[256]{0:T(256)S(1)}, ...), condition=%wide.region_3.4_spmd, body=%wide.region_2.3_spmd.sunk | while | flops 16418 | bytes 266713 | solution.py:44
  553.0 19.7 %multiply_subtract_fusion.125 = (f32[256]{0:T(256)S(1)}, f32[256]{0:T(256)S(1)}, f32[256]{0:T(256)S(1)}, f32[256]{0:T(256)S(1)}, f32[256]{0:T(256)S(1)}, /*index...) fusion(f32[256]{0:T(256)S(1)} %bitcast.1266, ...), kind=kLoop, calls=%fused_computation.103.clone.1 | loop fusion | flops 16384 | bytes 66688 | tf_op jit(solution)/shard_map/while/body/eval_jaxpr/sub | solution.py:44
  574.6 19.7 %multiply_subtract_fusion.125 = (f32[256]{0:T(256)S(1)}, f32[256]{0:T(256)S(1)}, f32[256]{0:T(256)S(1)}, f32[256]{0:T(256)S(1)}, f32[256]{0:T(256)S(1)}, /*index...) fusion(f32[256]{0:T(256)S(1)} %bitcast.1266, ...), kind=kLoop, calls=%fused_computation.103.clone.1 | loop fusion | flops 16384 | bytes 66688 | tf_op jit(solution)/shard_map/while/body/eval_jaxpr/sub | solution.py:44
  596.1 19.7 %multiply_subtract_fusion.125 = (f32[256]{0:T(256)S(1)}, f32[256]{0:T(256)S(1)}, f32[256]{0:T(256)S(1)}, f32[256]{0:T(256)S(1)}, f32[256]{0:T(256)S(1)}, /*index...) fusion(f32[256]{0:T(256)S(1)} %bitcast.1266, ...), kind=kLoop, calls=%fused_computation.103.clone.1 | loop fusion | flops 16384 | bytes 66688 | tf_op jit(solution)/shard_map/while/body/eval_jaxpr/sub | solution.py:44
  617.7 19.7 %multiply_subtract_fusion.125 = (f32[256]{0:T(256)S(1)}, f32[256]{0:T(256)S(1)}, f32[256]{0:T(256)S(1)}, f32[256]{0:T(256)S(1)}, f32[256]{0:T(256)S(1)}, /*index...) fusion(f32[256]{0:T(256)S(1)} %bitcast.1266, ...), kind=kLoop, calls=%fused_computation.103.clone.1 | loop fusion | flops 16384 | bytes 66688 | tf_op jit(solution)/shard_map/while/body/eval_jaxpr/sub | solution.py:44
  639.2 19.7 %multiply_subtract_fusion.125 = (f32[256]{0:T(256)S(1)}, f32[256]{0:T(256)S(1)}, f32[256]{0:T(256)S(1)}, f32[256]{0:T(256)S(1)}, f32[256]{0:T(256)S(1)}, /*index...) fusion(f32[256]{0:T(256)S(1)} %bitcast.1266, ...), kind=kLoop, calls=%fused_computation.103.clone.1 | loop fusion | flops 16384 | bytes 66688 | tf_op jit(solution)/shard_map/while/body/eval_jaxpr/sub | solution.py:44
  660.8 19.7 %multiply_subtract_fusion.125 = (f32[256]{0:T(256)S(1)}, f32[256]{0:T(256)S(1)}, f32[256]{0:T(256)S(1)}, f32[256]{0:T(256)S(1)}, f32[256]{0:T(256)S(1)}, /*index...) fusion(f32[256]{0:T(256)S(1)} %bitcast.1266, ...), kind=kLoop, calls=%fused_computation.103.clone.1 | loop fusion | flops 16384 | bytes 66688 | tf_op jit(solution)/shard_map/while/body/eval_jaxpr/sub | solution.py:44
  682.4 19.7 %multiply_subtract_fusion.125 = (f32[256]{0:T(256)S(1)}, f32[256]{0:T(256)S(1)}, f32[256]{0:T(256)S(1)}, f32[256]{0:T(256)S(1)}, f32[256]{0:T(256)S(1)}, /*index...) fusion(f32[256]{0:T(256)S(1)} %bitcast.1266, ...), kind=kLoop, calls=%fused_computation.103.clone.1 | loop fusion | flops 16384 | bytes 66688 | tf_op jit(solution)/shard_map/while/body/eval_jaxpr/sub | solution.py:44
  702.3 19.1 %multiply_subtract_fusion.32 = (f32[256]{0:T(256)S(1)}, f32[256]{0:T(256)S(1)}, f32[256]{0:T(256)S(1)}, f32[256]{0:T(256)S(1)}, f32[256]{0:T(256)S(1)}, /*index=...) fusion(f32[256]{0:T(256)S(1)} %bitcast.1364, ...), kind=kLoop, calls=%fused_computation.274 | loop fusion | flops 15872 | bytes 64636 | tf_op jit(solution)/shard_map/eval_jaxpr/sub | solution.py:44
  729.3 9.1 copy.197
  740.1 25.2 %pad_slice_fusion.3 = (f32[5,256,6,256]{1,3,2,0:T(8,128)}, f32[5,256,6,256]{1,3,2,0:T(8,128)}, f32[5,256,6,256]{1,3,2,0:T(8,128)}, f32[5,256,6,256]{1,3,2,0:T(8,128)}) fusion(f32[5,256,6,256]{1,3,2,0:T(8,128)} %copy.197), kind=kLoop, calls=%fused_computation.140 | loop fusion | bytes 39321600 | tf_op jit(solution)/shard_map/slice | solution.py:53
  775.4 16.3 %fusion.1 = f32[5,252,6,256]{1,3,2,0:T(8,128)} fusion(f32[5,256,6,256]{1,3,2,0:T(8,128)} %get-tuple-element.521, f32[5,256,6,256]{1,3,2,0:T(8,128)} %get-tuple-element.520, f32[5,256,6,256]{1,3,2,0:T(8,128)} %get-tuple-element.519, f32[5,256,6,256]{1,3,2,0:T(8,128)} %get-tuple-element.518), kind=kLoop, calls=%fused_computation.157 | loop fusion | flops 9676800 | bytes 38707200 | tf_op jit(solution)/shard_map/add | solution.py:58
  791.7 17.8 %concatenate.55 = f32[5,256,6,256]{1,3,2,0:T(8,128)} concatenate(f32[5,1,6,256]{1,3,2,0:T(8,128)} %copy.198, f32[5,1,6,256]{1,3,2,0:T(8,128)} %copy.199, f32[5,252,6,256]{1,3,2,0:T(8,128)} %fusion.1, f32[5,1,6,256]{1,3,2,0:T(8,128)} %copy.200, f32[5,1,6,256]{1,3,2,0:T(8,128)} %copy.201), dimensions={1} | concatenate | bytes 15728640 | tf_op jit(solution)/shard_map/concatenate | solution.py:66
  809.4 10.5 convolution_bitcast_fusion
  820.0 10.4 copy.202
  894.6 9.5 fusion.5
  904.1 11.4 concatenate.62
  937.4 11.6 fusion.68
  948.9 11.3 fusion.69
  960.2 35.8 %fusion.8 = f32[3,32,48,256]{3,2,1,0:T(8,128)} fusion(f32[3,32,48,256]{3,1,2,0:T(8,128)} %get-tuple-element.529, f32[3,32,48,256]{3,1,2,0:T(8,128)} %get-tuple-element.526, f32[3,32,48,256]{3,1,2,0:T(8,128)} %get-tuple-element.528, f32[3,32,48,256]{3,1,2,0:T(8,128)} %get-tuple-element.525, f32[3,32,48,256]{3,1,2,0:T(8,128)} %get-tuple-element.527, ...), kind=kLoop, calls=%fused_computation.176 | loop fusion | flops 9437184 | bytes 33030144 | tf_op jit(solution)/shard_map/add | solution.py:75
  996.0 67.9 %all-to-all-done.1 = f32[5,256,6,256]{3,2,0,1:T(8,128)} async-done(((f32[5,256,6,256]{3,2,0,1:T(8,128)}), f32[5,256,6,256]{3,2,0,1:T(8,128)}, u32[]{:S(2)}, u32[]{:S(2)}) %all-to-all-start.1) | async-done | bytes 7864352 | tf_op jit(solution)/shard_map/all_to_all | solution.py:86
  1077.6 11.4 fusion.30
  1135.0 134.4 %reduce-scatter.4.cloned.1.call-done = f32[16,64]{1,0:T(8,128)} async-done(((f32[512,64]{1,0:T(8,128)}), f32[16,64]{1,0:T(8,128)}) %reduce-scatter.4.cloned.1.call-update) | async-done | bytes 4112
  (282 shorter events, 233.4 us)
Async XLA Ops:
  11.1 3.1 copy-start
  21.8 699.7 %all-to-all-start = ((f32[5,32,48,256]{3,1,0,2:T(8,128)}), f32[5,32,48,256]{3,1,0,2:T(8,128)}, u32[]{:S(2)}, u32[]{:S(2)}) async-start(f32[5,32,48,256]{3,1,0,2:T(8,128)} %copy.194), calls=%async_computation | async-start | bytes 15728640 | tf_op jit(solution)/shard_map/all_to_all | solution.py:82
  830.4 233.5 %all-to-all-start.1 = ((f32[5,256,6,256]{3,2,0,1:T(8,128)}), f32[5,256,6,256]{3,2,0,1:T(8,128)}, u32[]{:S(2)}, u32[]{:S(2)}) async-start(f32[5,256,6,256]{3,2,0,1:T(8,128)} %copy.202), calls=%async_computation.1 | async-start | bytes 20971520 | tf_op jit(solution)/shard_map/all_to_all | solution.py:86
  836.4 433.0 %reduce-scatter.4.cloned.1.call-start = ((), (), s32[]{:S(2)}) async-start(), calls=%async_computation.3 | async-start | bytes 270336
  839.1 6.7 copy-start.1
  839.1 6.7 copy-start.3
  840.1 85.1 %collective-permute-start.1 = (f32[3,32,3,256]{3,1,2,0:T(8,128)}, f32[3,32,3,256]{3,1,2,0:T(8,128)}, u32[]{:S(2)}, u32[]{:S(2)}) collective-permute-start(f32[3,32,3,256]{3,1,2,0:T(8,128)} %copy.285), channel_id=1, source_target_pairs={{0,1},{1,2},{2,3},{4,5},{5,6},{6,7},{8,9},{9,10},{10,11},{12,13},{... | collective-permute-start | bytes 884744 | tf_op jit(solution)/shard_map/ppermute | solution.py:19
  843.0 92.7 %collective-permute-start = (f32[3,32,3,256]{3,1,2,0:T(8,128)}, f32[3,32,3,256]{3,1,2,0:T(8,128)}, u32[]{:S(2)}, u32[]{:S(2)}) collective-permute-start(f32[3,32,3,256]{3,1,2,0:T(8,128)} %copy.286), channel_id=1, source_target_pairs={{1,0},{2,1},{3,2},{5,4},{6,5},{7,6},{9,8},{10,9},{11,10},{13,12},{... | collective-permute-start | bytes 884744 | tf_op jit(solution)/shard_map/ppermute | solution.py:22
  845.8 2.2 copy-start.2
  904.1 11.4 copy-start.14
  904.1 11.5 copy-start.12
  904.1 11.5 copy-start.13
  916.2 8.3 copy-start.8
  1063.9 11.3 slice-start.4
  1070.5 4.7 slice-start.2
  1070.5 4.7 slice-start.5
  1071.9 3.3 slice-start
  1071.9 4.6 slice-start.3
  1072.3 4.9 slice-start.1
  1072.3 5.3 copy-start.4
  1120.8 2.7 copy-start.5
  1123.5 2.6 copy-start.7
  1123.5 2.6 copy-start.9
  1123.5 2.6 copy-start.10
  1123.5 2.7 copy-start.11
  1123.5 3.1 copy-start.6
Sparse Core Ops, SparseCore 0:
  1135.1 134.2 reduce-scatter.3
where the time goes:
time: 1290 us; the launch traced here: 1280 us
  other arithmetic  432 us (33%)
  loops' own time  289 us (22%)
  local copies, waits for them, and re-layouts  264 us (20%)
  waiting for transfers between devices  202 us (16%)
  between operations  53.1 us (4%)
  matrix products  18.8 us (1%)
  starting transfers between devices  17 us (1%)
    another operation x2, loops' own time, inverse_of(): lax.linalg.tridiagonal_solve(lower, middle, upper, jnp.eye(count, dtype=j...  289 us
    div x8, other arithmetic, inverse_of(): lax.linalg.tridiagonal_solve(lower, middle, upper, jnp.eye(count, dtype=j...  161 us
    sub x8, other arithmetic, inverse_of(): lax.linalg.tridiagonal_solve(lower, middle, upper, jnp.eye(count, dtype=j...  157 us
    unnamed x2, waiting for transfers between devices  134 us
    all_to_all x1, waiting for transfers between devices, transposed_x(): return lax.all_to_all(solved, 'gx', split_axis=1, concat_axis=2, tiled=True)  67.9 us
    unnamed x54, local copies, waits for them, and re-layouts  38.1 us
    slice x85, local copies, waits for them, and re-layouts, inverse_of(): lax.linalg.tridiagonal_solve(lower, middle, upper, jnp.eye(count, dtype=j...  37.6 us
    add x1, other arithmetic, explicit_y(): 0.75 * (take(1) - take(-1)) - 0.15 * (take(2) - take(-2))  35.8 us
  transfers between devices with their start and end apart: 5, of which 2 were waited for; matrix products, arithmetic and copies ran while one was open for 41% of the time, Pallas kernels for 0%

commit v1 on v0

v1 whole, which is shorter than its diff:
```python
import functools

import numpy as np
import jax
import jax.numpy as jnp
from jax import lax
from jax.experimental import pallas as pl
from jax.experimental.pallas import tpu as pltpu
from jax.sharding import PartitionSpec as P

BINS = 64
TILE = 8
TAPS = 5

time_step = 0.25
four_pi = 4.0 * 3.141592653589793
VMEM = pltpu.VMEM
SMEM = pltpu.SMEM


def diagonals(count):
    lower = np.full(count, 1.0 / 3.0)
    upper = np.full(count, 1.0 / 3.0)
    lower[1] = lower[count - 2] = upper[1] = upper[count - 2] = 0.25
    lower[0] = upper[count - 1] = 0.0
    lower[count - 1] = upper[0] = 2.0
    return lower, upper


def stencil(count):
    rows = np.zeros((count, count))
    for i in range(2, count - 2):
        rows[i, i + 1], rows[i, i - 1] = 7.0 / 9.0, -7.0 / 9.0
        rows[i, i + 2], rows[i, i - 2] = 1.0 / 36.0, -1.0 / 36.0
    rows[0, :3] = (-2.5, 2.0, 0.5)
    rows[1, 0], rows[1, 2] = -0.75, 0.75
    rows[count - 2, count - 3], rows[count - 2, count - 1] = -0.75, 0.75
    rows[count - 1, count - 3:] = (-0.5, -2.0, 2.5)
    return rows


def dense_derivative(count):
    lower, upper = diagonals(count)
    matrix = np.eye(count) + np.diag(lower[1:], -1) + np.diag(upper[:-1], 1)
    return np.linalg.solve(matrix, stencil(count))


def x_tables(blocks, cells):
    count = blocks * cells
    lower, upper = diagonals(count)
    rows = stencil(count)
    down, pivot = np.zeros(count), np.ones(count)
    for i in range(1, count):
        down[i] = lower[i] / pivot[i - 1]
        pivot[i] = 1.0 - down[i] * upper[i - 1]
    up, pivot_up = np.zeros(count), np.ones(count)
    for i in range(count - 2, -1, -1):
        up[i] = upper[i] / pivot_up[i + 1]
        pivot_up[i] = 1.0 - up[i] * lower[i + 1]
    from_left = rows.copy()
    for i in range(1, count):
        from_left[i] -= down[i] * from_left[i - 1]
    from_right = rows.copy()
    for i in range(count - 2, -1, -1):
        from_right[i] -= up[i] * from_right[i + 1]
    weights = np.zeros((blocks, 2, cells))
    chain = np.zeros((blocks, 2))
    sweep = np.zeros((blocks, 3, cells))
    taps = np.zeros((blocks, 4, TAPS))
    ends = np.zeros((blocks, 4))
    for d in range(blocks):
        s, e = d * cells, (d + 1) * cells
        if d < blocks - 1:
            weights[d, 0] = from_left[e + 1, s:e]
            chain[d, 0] = np.prod(-down[s + 2:e + 2])
        if d > 0:
            weights[d, 1] = from_right[s - 2, s:e]
            chain[d, 1] = np.prod(-up[s - 2:e - 2])
        sweep[d, 0] = down[s:e]
        sweep[d, 1] = 1.0 / pivot[s:e]
        sweep[d, 2] = upper[s:e] / pivot[s:e]
        sweep[d, 1, -1] = 1.0 / (pivot[e - 1] + pivot_up[e - 1] - 1.0)
        taps[d, 0, 2:] = from_left[s, s:s + 3]
        taps[d, 3, :3] = from_right[e - 1, e - 3:e]
        for k in range(-2, 3):
            if 0 <= s + 1 + k:
                taps[d, 1, k + 2] = rows[s + 1, s + 1 + k]
            if e - 2 + k < count:
                taps[d, 2, k + 2] = rows[e - 2, e - 2 + k]
        ends[d, 0] = -1.0 / down[s + 1]
        ends[d, 1] = taps[d, 1, 1] / down[s + 1] if d > 0 else 0.0
        ends[d, 2] = -1.0 / up[e - 2]
        ends[d, 3] = taps[d, 2, 3] / up[e - 2] if d < blocks - 1 else 0.0
        if d > 0:
            ends[d, 1] = rows[s + 1, s - 1] / down[s + 1]
        if d < blocks - 1:
            ends[d, 3] = rows[e - 2, e] / up[e - 2]
    largest, hops, reach = np.abs(chain).max(), 1, np.abs(chain).max()
    while hops < blocks - 1 and reach >= np.finfo(np.float32).tiny:
        hops, reach = hops + 1, reach * largest
    edges = np.concatenate([taps.reshape(blocks, -1), ends], 1)
    return (
        weights.astype(np.float32),
        chain.astype(np.float32),
        sweep.astype(np.float32),
        edges.astype(np.float32),
        hops,
    )


def sums_kernel(cells, weights_ref, state_ref, flow_ref, right_ref, left_ref):
    def load(f, i):
        return flow_ref[i] if f == 4 else state_ref[f, i]

    for f in range(5):
        total_right = weights_ref[0, 0] * load(f, 0)
        total_left = weights_ref[1, 0] * load(f, 0)
        for i in range(1, cells):
            value = load(f, i)
            total_right += weights_ref[0, i] * value
            total_left += weights_ref[1, i] * value
        right_ref[0, f] = total_right
        left_ref[0, f] = total_left
        right_ref[1, f] = load(f, cells - 1)
        left_ref[1, f] = load(f, 0)


def main_kernel(
    cells, width, depth,
    row_ref, sweep_ref, edges_ref,
    state_ref, flow_ref, right_ref, left_ref, low_ref, high_ref,
    zhi_ref, zlo_ref, along_z_ref, normal_ref, pos_ref, observer_ref, bin_ref,
    next_ref, signal_ref,
    wide, swept, zrate, rate, picked,
):
    step = pl.program_id(0)
    rows = pl.ds(pl.multiple_of(step * TILE, TILE), TILE)
    window = pl.ds(pl.multiple_of(step * TILE, TILE), 3 * TILE)

    def load(f, i):
        return flow_ref[i, rows, :] if f == 4 else state_ref[f, i, rows, :]

    @pl.when(step == 0)
    def _():
        def widen(i, carry):
            for slot, f in enumerate((0, 2, 4)):
                body = flow_ref[i] if f == 4 else state_ref[f, i]
                wide[slot, i, TILE:TILE + width, :] = body
                wide[slot, i, TILE - 3:TILE, :] = low_ref[slot, i]
                wide[slot, i, TILE + width:TILE + width + 3, :] = high_ref[slot, i]
            return carry
        lax.fori_loop(0, cells, widen, 0)

    for slot, f in enumerate((0, 3, 4)):
        block = flow_ref[:, rows, :] if f == 4 else state_ref[f, :, rows, :]
        block = block.reshape(cells * TILE, depth)
        high = block.astype(jnp.bfloat16)
        rest = (block - high.astype(jnp.float32)).astype(jnp.bfloat16)
        out = jnp.dot(rest, zhi_ref[...], preferred_element_type=jnp.float32)
        out += jnp.dot(high, zlo_ref[...], preferred_element_type=jnp.float32)
        out += jnp.dot(high, zhi_ref[...], preferred_element_type=jnp.float32)
        zrate[slot] = out.reshape(cells, TILE, depth)

    fields = range(5)

    def tap(k, position):
        return edges_ref[0, k * TAPS + position + 2]

    def end(k):
        return edges_ref[0, 4 * TAPS + k]

    carry = []
    for f in fields:
        first = tap(0, 0) * load(f, 0) + tap(0, 1) * load(f, 1) + tap(0, 2) * load(f, 2)
        value = first + end(0) * right_ref[0, f] + end(1) * right_ref[1, f]
        swept[f, 0] = value
        second = (
            tap(1, -1) * load(f, 0) + tap(1, 0) * load(f, 1)
            + tap(1, 1) * load(f, 2) + tap(1, 2) * load(f, 3) + tap(1, -2) * right_ref[1, f]
        )
        value = second - sweep_ref[0, 1] * value
        swept[f, 1] = value
        carry.append(value)

    def forward(i, carry):
        new = []
        factor = sweep_ref[0, i]
        for f in fields:
            rhs = 7.0 / 9.0 * (load(f, i + 1) - load(f, i - 1)) + 1.0 / 36.0 * (
                load(f, i + 2) - load(f, i - 2)
            )
            value = rhs - factor * carry[f]
            swept[f, i] = value
            new.append(value)
        return tuple(new)

    carry = lax.fori_loop(2, cells - 2, forward, tuple(carry), unroll=2)
    solved = []
    n = cells
    for f in fields:
        before = (
            tap(2, -2) * load(f, n - 4) + tap(2, -1) * load(f, n - 3) + tap(2, 0) * load(f, n - 2)
            + tap(2, 1) * load(f, n - 1) + tap(2, 2) * left_ref[1, f]
        )
        value = before - sweep_ref[0, n - 2] * carry[f]
        swept[f, n - 2] = value
        last = (
            tap(3, -2) * load(f, n - 3) + tap(3, -1) * load(f, n - 2) + tap(3, 0) * load(f, n - 1)
            + end(2) * left_ref[0, f] + end(3) * left_ref[1, f]
        )
        solved.append((last - sweep_ref[0, n - 1] * value) * sweep_ref[1, n - 1])

    def y_rate(slot, i):
        whole = wide[slot, i, window, :]

        def take(shift):
            return whole[TILE + shift:2 * TILE + shift]

        return (
            0.75 * (take(1) - take(-1))
            - 0.15 * (take(2) - take(-2))
            + 1.0 / 60.0 * (take(3) - take(-3))
        )

    def finish(i, x):
        p, u, v, w, flow = (load(f, i) for f in fields)
        rates = (
            -(flow * x[0] + x[1] + y_rate(1, i) + zrate[1, i]),
            -(flow * x[1] + u * x[4] + v * y_rate(2, i) + w * zrate[2, i] + x[0]),
            -(flow * x[2] + y_rate(0, i)),
            -(flow * x[3] + zrate[0, i]),
        )
        place = pl.ds(pl.multiple_of(i * width + step * TILE, TILE), TILE)
        for c, old in enumerate((p, u, v, w)):
            rate[c, place, :] = rates[c]
            new = old + time_step * rates[c]
            next_ref[c, i] = new
            if c == 0:
                rate[4, place, :] = new

    finish(n - 1, solved)

    def backward(k, carry):
        i = n - 2 - k
        x = tuple(
            swept[f, i] * sweep_ref[1, i] - sweep_ref[2, i] * carry[f] for f in fields
        )
        finish(i, x)
        return x

    lax.fori_loop(0, n - 1, backward, tuple(solved))

    @pl.when(step == pl.num_programs(0) - 1)
    def _():
        faces = picked.shape[1]

        def pick(k, carry):
            row = row_ref[0, k]
            for c in range(5):
                picked[c, pl.ds(k, 1), :] = rate[c, pl.ds(row, 1), :]
            return carry

        lax.fori_loop(0, faces, pick, 0, unroll=4)
        mask = lax.broadcasted_iota(jnp.int32, (faces, depth), 1) == along_z_ref[...]
        at = [
            jnp.sum(jnp.where(mask, picked[c], 0.0), axis=1, keepdims=True) for c in range(5)
        ]
        normal = [normal_ref[:, c:c + 1] for c in range(3)]
        normal_rate = normal[0] * at[1] + normal[1] * at[2] + normal[2] * at[3]
        offset = [observer_ref[c:c + 1, :] - pos_ref[:, c:c + 1] for c in range(3)]
        distance = jnp.sqrt(
            offset[0] * offset[0] + offset[1] * offset[1] + offset[2] * offset[2]
        )
        normal_r = (
            normal[0] * offset[0] + normal[1] * offset[1] + normal[2] * offset[2]
        ) / distance
        contribution = (normal_rate + (at[0] + at[4] / distance) * normal_r) / (
            four_pi * distance
        )
        bins = bin_ref[...]

        def gather(b, carry):
            signal_ref[pl.ds(b, 1), :] = jnp.sum(
                jnp.where(bins == b, contribution, 0.0), axis=0, keepdims=True
            )
            return carry

        lax.fori_loop(0, BINS, gather, 0, unroll=2)


def per_device(sizes, state, mean_flow, face_cell, face_normal, face_pos, observer_pos, time_bin):
    blocks, groups = sizes
    _, cells, width, depth = state.shape
    faces, observers = time_bin.shape
    tiles = width // TILE
    block, group = lax.axis_index("gx"), lax.axis_index("yz")
    weights, chain, sweep, edges, hops = x_tables(blocks, cells)

    def mine(table):
        return lax.dynamic_index_in_dim(jnp.asarray(table), block, 0, keepdims=False)

    params = dict(vmem_limit_bytes=60 * 1024 * 1024)
    plane = jax.ShapeDtypeStruct((2, 5, width, depth), jnp.float32)
    plane_spec = pl.BlockSpec((2, 5, TILE, depth), lambda j: (0, 0, j, 0))
    to_right, to_left = pl.pallas_call(
        functools.partial(sums_kernel, cells),
        grid=(tiles,),
        out_shape=(plane, plane),
        in_specs=[
            pl.BlockSpec(memory_space=SMEM),
            pl.BlockSpec((4, cells, TILE, depth), lambda j: (0, 0, j, 0)),
            pl.BlockSpec((cells, TILE, depth), lambda j: (0, j, 0)),
        ],
        out_specs=(plane_spec, plane_spec),
        compiler_params=pltpu.CompilerParams(**params),
    )(mine(weights), state, mean_flow)

    def neighbours(count):
        up = [(i, i + 1) for i in range(count - 1)]
        return up, [(b, a) for a, b in up]

    up, down = neighbours(groups)
    crossing = lambda a, b: jnp.stack(
        [state[0, :, a:b], state[2, :, a:b], mean_flow[:, a:b]]
    )
    low = lax.ppermute(crossing(width - 3, width), "yz", up)
    high = lax.ppermute(crossing(0, 3), "yz", down)
    up, down = neighbours(blocks)
    from_left = lax.ppermute(to_right, "gx", up)
    from_right = lax.ppermute(to_left, "gx", down)
    own = mine(chain)
    sum_left, sum_right = from_left[0], from_right[0]
    for _ in range(hops - 1):
        sum_left = lax.ppermute(to_right[0] + own[0] * sum_left, "gx", up)
        sum_right = lax.ppermute(to_left[0] + own[1] * sum_right, "gx", down)
    from_left = jnp.stack([sum_left, from_left[1]])
    from_right = jnp.stack([sum_right, from_right[1]])

    operator = dense_derivative(depth).T.astype(np.float32)
    z_high = jnp.asarray(operator).astype(jnp.bfloat16)
    z_low = (jnp.asarray(operator) - z_high.astype(jnp.float32)).astype(jnp.bfloat16)

    planes = width * groups
    along_x = face_cell // (planes * depth) - block * cells
    along_y = face_cell // depth % planes - group * width
    along_z = face_cell % depth
    row = (along_x * width + along_y).reshape(1, faces)

    def whole(*shape):
        return pl.BlockSpec(shape, lambda j: (0,) * len(shape))

    smem = pl.BlockSpec(memory_space=SMEM)
    state_next, signal = pl.pallas_call(
        functools.partial(main_kernel, cells, width, depth),
        grid=(tiles,),
        out_shape=(
            jax.ShapeDtypeStruct(state.shape, jnp.float32),
            jax.ShapeDtypeStruct((BINS, observers), jnp.float32),
        ),
        in_specs=[
            smem, smem, smem,
            whole(4, cells, width, depth), whole(cells, width, depth),
            plane_spec, plane_spec,
            whole(3, cells, 3, depth), whole(3, cells, 3, depth),
            whole(depth, depth), whole(depth, depth),
            whole(faces, 1), whole(faces, 3), whole(faces, 3),
            whole(3, observers), whole(faces, observers),
        ],
        out_specs=(
            pl.BlockSpec((4, cells, TILE, depth), lambda j: (0, 0, j, 0)),
            whole(BINS, observers),
        ),
        scratch_shapes=[
            VMEM((3, cells, width + 2 * TILE, depth), jnp.float32),
            VMEM((5, cells, TILE, depth), jnp.float32),
            VMEM((3, cells, TILE, depth), jnp.float32),
            VMEM((5, cells * width, depth), jnp.float32),
            VMEM((5, faces, depth), jnp.float32),
        ],
        compiler_params=pltpu.CompilerParams(**params),
    )(
        row, mine(sweep), mine(edges.reshape(blocks, 1, -1)),
        state, mean_flow, from_left, from_right, low, high,
        z_high, z_low, along_z.reshape(faces, 1), face_normal.T, face_pos.T,
        observer_pos, time_bin,
    )
    devices = blocks * groups
    pieces = signal.T.reshape(devices, -1)
    pieces = lax.all_to_all(pieces, ("gx", "yz"), split_axis=0, concat_axis=0, tiled=True)
    signal = jnp.sum(pieces.reshape(devices, -1), axis=0).reshape(observers // devices, BINS)
    return state_next, signal


def solution(mesh):
    in_specs = (
        P(None, "gx", "yz", None),
        P("gx", "yz", None),
        P(("gx", "yz")),
        P(None, ("gx", "yz")),
        P(None, ("gx", "yz")),
        P(),
        P(("gx", "yz"), None),
    )
    out_specs = (P(None, "gx", "yz", None), P(("gx", "yz"), None))
    sizes = (mesh.shape["gx"], mesh.shape["yz"])
    return jax.shard_map(
        functools.partial(per_device, sizes),
        mesh=mesh, in_specs=in_specs, out_specs=out_specs, check_vma=False,
    )
```

time: 1290 us -> 109 us (0.08); the launches traced: 1280 us -> 109 us
  other arithmetic: 432 us -> 8.84 us
  loops' own time: 289 us -> 0 us
  local copies, waits for them, and re-layouts: 264 us -> 12.5 us
  waiting for transfers between devices: 202 us -> 22.4 us
  between operations: 53.1 us -> 0.83 us
  Pallas kernels: 0 us -> 32 us
  matrix products: 18.8 us -> 0 us
    another operation x2 -> x0, loops' own time: 289 us -> none  [inverse_of(): lax.linalg.tridiagonal_solve(lower, middle, upper, jnp.eye(count, dtype=j...]
    div x9 -> x0, other arithmetic: 161 us -> none  [the longest x8 161 us: inverse_of(): lax.linalg.tridiagonal_solve(lower, middle, upper, jnp.eye(count, dtype=j...]
    sub x8 -> x0, other arithmetic: 157 us -> none  [inverse_of(): lax.linalg.tridiagonal_solve(lower, middle, upper, jnp.eye(count, dtype=j...]
    unnamed x2 -> x0, waiting for transfers between devices: 134 us -> none
    slice x103 -> x4, local copies, waits for them, and re-layouts: 104 us -> 1.91 us  [the longest x1 1.29 us: per_device(): state[0, :, a:b]]
    all_to_all x2 -> x0, waiting for transfers between devices: 67.9 us -> none  [the longest x1 67.9 us: transposed_x(): return lax.all_to_all(solved, 'gx', split_axis=1, concat_axis=2, tiled=True)]
    add x5 -> x4, other arithmetic: 66 us -> 6.32 us  [the longest x2 3.26 us: per_device(): sum_right = lax.ppermute(to_left[0] + own[1] * sum_right, 'gx', down)]
    concatenate x28 -> x0, local copies, waits for them, and re-layouts: 46.4 us -> none  [the longest x2 29.2 us: compact_rhs(): jnp.concatenate([first_row, second_row, middle_rows, before_last, last_ro...]
  transfers between devices with their start and end apart: 5 -> 8, of which waited for: 2 -> 3; matrix products, arithmetic and copies ran while one was open for 41% -> 16% of each run, Pallas kernels for 0% -> 0%
where the time goes in v1:
time: 109 us
  Pallas kernels  32 us (29%)
  waiting for transfers between devices  22.4 us (21%)
  starting transfers between devices  20.2 us (19%)
  local copies, waits for them, and re-layouts  12.5 us (11%)
  blocking collectives  11.7 us (11%)
  other arithmetic  8.84 us (8%)
    pallas_call x1, Pallas kernels, per_device(): pl.pallas_call(functools.partial(main_kernel, cells, width, depth), grid=...  25.9 us
    ppermute x1, waiting for transfers between devices, per_device(): from_left = lax.ppermute(to_right, 'gx', up)  14.3 us
    all_to_all x1, blocking collectives, per_device(): lax.all_to_all(pieces, ('gx', 'yz'), split_axis=0, concat_axis=0, tiled=T...  11.7 us
    ppermute x2, starting transfers between devices, per_device(): sum_left = lax.ppermute(to_right[0] + own[0] * sum_left, 'gx', up)  8.7 us
    ppermute x2, waiting for transfers between devices, per_device(): sum_left = lax.ppermute(to_right[0] + own[0] * sum_left, 'gx', up)  6.96 us
    pallas_call x1, Pallas kernels, per_device(): pl.pallas_call(functools.partial(sums_kernel, cells), grid=(tiles,), out_...  6.13 us
    ppermute x1, starting transfers between devices, per_device(): from_left = lax.ppermute(to_right, 'gx', up)  4.89 us
    squeeze x3, local copies, waits for them, and re-layouts, mine(): lax.dynamic_index_in_dim(jnp.asarray(table), block, 0, keepdims=False)  3.73 us
  transfers between devices with their start and end apart: 8, of which 3 were waited for; matrix products, arithmetic and copies ran while one was open for 16% of the time, Pallas kernels for 0%

profile of v1, /device:TPU:0, one launch (start us, length us, event | category | flops | bytes accessed | tf_op | source)
XLA Modules:
  0.0 108.5 jit_solution(18069373953689009306)
XLA Ops:
  0.6 1.2 %dynamic-slice_bitcast_fusion.1.weights_ref = f32[2,32]{1,0:T(2,128)} fusion(f32[8,2,32]{2,1,0:T(2,128)} %constant.84.clone, s32[]{:T(128)S(6)} %select_n.32), kind=kLoop, calls=%fused_computation.24 | loop fusion | bytes 516 | tf_op jit(solution)/shard_map/jit(dynamic_index_in_dim)/squeeze | solution.py:300
  1.9 6.1 %shard_map.131 = (f32[2,5,48,256]{3,2,1,0:T(8,128)}, f32[2,5,48,256]{3,2,1,0:T(8,128)}) custom-call(f32[2,32]{1,0:T(2,128)} %dynamic-slice_bitcast_fusion.1.weights_ref, f32[4,32,48,256]{3,2,1,0:T(8,128)} %state_ref.3, f32[32,48,256]{2,1,0:T(8,128)} %flow_ref.3), custom_call_target="tpu_custom_call" | custom-call | tf_op jit(solution)/shard_map/pallas_call | solution.py:305
  8.0 4.9 %collective-permute-start = (f32[2,5,48,256]{3,2,1,0:T(8,128)}, f32[2,5,48,256]{3,2,1,0:T(8,128)S(1)}, u32[]{:S(2)}, u32[]{:S(2)}) collective-permute-start(f32[2,5,48,256]{3,2,1,0:T(8,128)} %get-tuple-element.6), channel_id=1, source_target_pairs={{0,4},{4,8},{8,12},{12,16},{16,20},{20,24},{24,28},{1,5},{5,9},{9,... | collective-permute-start | bytes 1474568 | tf_op jit(solution)/shard_map/ppermute | solution.py:329
  12.9 1.3 %fusion.7 = (f32[1,32,3,256]{3,2,1,0:T(4,128)S(1)}, f32[1,32,3,256]{3,2,1,0:T(4,128)S(1)}, f32[1,32,3,256]{3,2,1,0:T(4,128)S(1)}, f32[1,32,3,256]{3,2,1,0:T(4,128)S(1)}) fusion(f32[4,32,48,256]{3,2,1,0:T(8,128)} %state_ref.3), kind=kLoop, calls=%fused_computation.30 | loop fusion | bytes 786432 | tf_op jit(solution)/shard_map/slice | solution.py:324
  14.2 1.1 slice_bitcast_fusion
  15.4 1.5 %collective-permute-start.6 = (f32[3,32,3,256]{3,2,1,0:T(4,128)S(1)}, f32[3,32,3,256]{3,2,1,0:T(4,128)S(1)}, u32[]{:S(2)}, u32[]{:S(2)}) collective-permute-start(f32[3,32,3,256]{3,2,1,0:T(4,128)S(1)} %pad_maximum_fusion.2), channel_id=1, source_target_pairs={{0,1},{1,2},{2,3},{4,5},{5,6},{6,7},{8,9},{9,10},{10,11},{12,13},{... | collective-permute-start | bytes 884744 | tf_op jit(solution)/shard_map/ppermute | solution.py:326
  16.9 1.3 %collective-permute-start.3 = (f32[2,5,48,256]{3,2,1,0:T(8,128)}, f32[2,5,48,256]{3,2,1,0:T(8,128)S(1)}, u32[]{:S(2)}, u32[]{:S(2)}) collective-permute-start(f32[2,5,48,256]{3,2,1,0:T(8,128)} %get-tuple-element.7), channel_id=1, source_target_pairs={{4,0},{8,4},{12,8},{16,12},{20,16},{24,20},{28,24},{5,1},{9,5},{13... | collective-permute-start | bytes 1474568 | tf_op jit(solution)/shard_map/ppermute | solution.py:330
  18.3 1.3 %collective-permute-start.7 = (f32[3,32,3,256]{3,2,1,0:T(4,128)S(1)}, f32[3,32,3,256]{3,2,1,0:T(4,128)S(1)}, u32[]{:S(2)}, u32[]{:S(2)}) collective-permute-start(f32[3,32,3,256]{3,2,1,0:T(4,128)S(1)} %pad_maximum_fusion.3), channel_id=1, source_target_pairs={{1,0},{2,1},{3,2},{5,4},{6,5},{7,6},{9,8},{10,9},{11,10},{13,12},{... | collective-permute-start | bytes 884744 | tf_op jit(solution)/shard_map/ppermute | solution.py:327
  19.6 0.7 constant_dynamic-slice_fusion
  20.9 14.3 %collective-permute-done = f32[2,5,48,256]{3,2,1,0:T(8,128)S(1)} collective-permute-done((f32[2,5,48,256]{3,2,1,0:T(8,128)}, f32[2,5,48,256]{3,2,1,0:T(8,128)S(1)}, u32[]{:S(2)}, u32[]{:S(2)}) %collective-permute-start) | collective-permute-done | bytes 491552 | tf_op jit(solution)/shard_map/ppermute | solution.py:329
  35.2 1.5 %fusion.3 = f32[5,48,256]{2,1,0:T(8,128)S(1)} fusion(f32[2,5,48,256]{3,2,1,0:T(8,128)S(1)} %collective-permute-done, f32[2,5,48,256]{3,2,1,0:T(8,128)} %get-tuple-element.6, f32[]{:T(128)} %bitcast.5), kind=kLoop, calls=%fused_computation.9 | loop fusion | flops 122880 | bytes 737284 | tf_op jit(solution)/shard_map/add | solution.py:334
  36.7 4.3 %collective-permute-start.1 = (f32[5,48,256]{2,1,0:T(8,128)S(1)}, f32[5,48,256]{2,1,0:T(8,128)S(1)}, u32[]{:S(2)}, u32[]{:S(2)}) collective-permute-start(f32[5,48,256]{2,1,0:T(8,128)S(1)} %fusion.3), channel_id=1, source_target_pairs={{0,4},{4,8},{8,12},{12,16},{16,20},{20,24},{24,28},{1,5},{5,9},{9,... | collective-permute-start | bytes 737288 | tf_op jit(solution)/shard_map/ppermute | solution.py:334
  41.0 1.6 %fusion.1 = f32[5,48,256]{2,1,0:T(8,128)S(1)} fusion(f32[2,5,48,256]{3,2,1,0:T(8,128)S(1)} %collective-permute-done.3, f32[2,5,48,256]{3,2,1,0:T(8,128)} %get-tuple-element.7, f32[]{:T(128)} %bitcast.9), kind=kLoop, calls=%fused_computation.6 | loop fusion | flops 122880 | bytes 737284 | tf_op jit(solution)/shard_map/add | solution.py:335
  42.7 1.3 %collective-permute-start.4 = (f32[5,48,256]{2,1,0:T(8,128)S(1)}, f32[5,48,256]{2,1,0:T(8,128)S(1)}, u32[]{:S(2)}, u32[]{:S(2)}) collective-permute-start(f32[5,48,256]{2,1,0:T(8,128)S(1)} %fusion.1), channel_id=1, source_target_pairs={{4,0},{8,4},{12,8},{16,12},{20,16},{24,20},{28,24},{5,1},{9,5},{13... | collective-permute-start | bytes 737288 | tf_op jit(solution)/shard_map/ppermute | solution.py:335
  44.6 7.0 %collective-permute-done.1 = f32[5,48,256]{2,1,0:T(8,128)S(1)} collective-permute-done((f32[5,48,256]{2,1,0:T(8,128)S(1)}, f32[5,48,256]{2,1,0:T(8,128)S(1)}, u32[]{:S(2)}, u32[]{:S(2)}) %collective-permute-start.1) | collective-permute-done | bytes 245792 | tf_op jit(solution)/shard_map/ppermute | solution.py:334
  51.5 1.5 %bitcast_add_fusion.1 = f32[5,48,256]{2,1,0:T(8,128)S(1)} fusion(f32[5,48,256]{2,1,0:T(8,128)S(1)} %collective-permute-done.1, f32[2,5,48,256]{3,2,1,0:T(8,128)} %get-tuple-element.6, f32[]{:T(128)} %bitcast.5), kind=kLoop, calls=%fused_computation.11 | loop fusion | flops 122880 | bytes 737284 | tf_op jit(solution)/shard_map/add | solution.py:334
  53.0 4.4 %collective-permute-start.2 = (f32[5,48,256]{2,1,0:T(8,128)S(1)}, f32[5,48,256]{2,1,0:T(8,128)S(1)}, u32[]{:S(2)}, u32[]{:S(2)}) collective-permute-start(f32[5,48,256]{2,1,0:T(8,128)S(1)} %bitcast_add_fusion.1), channel_id=1, source_target_pairs={{0,4},{4,8},{8,12},{12,16},{16,20},{20,24},{24,28},{1,5},{5,9},{9,... | collective-permute-start | bytes 737288 | tf_op jit(solution)/shard_map/ppermute | solution.py:334
  57.5 1.6 %bitcast_add_fusion = f32[5,48,256]{2,1,0:T(8,128)S(1)} fusion(f32[5,48,256]{2,1,0:T(8,128)S(1)} %collective-permute-done.4, f32[2,5,48,256]{3,2,1,0:T(8,128)} %get-tuple-element.7, f32[]{:T(128)} %bitcast.9), kind=kLoop, calls=%fused_computation.10 | loop fusion | flops 122880 | bytes 737284 | tf_op jit(solution)/shard_map/add | solution.py:335
  59.1 1.3 %collective-permute-start.5 = (f32[5,48,256]{2,1,0:T(8,128)S(1)}, f32[5,48,256]{2,1,0:T(8,128)S(1)}, u32[]{:S(2)}, u32[]{:S(2)}) collective-permute-start(f32[5,48,256]{2,1,0:T(8,128)S(1)} %bitcast_add_fusion), channel_id=1, source_target_pairs={{4,0},{8,4},{12,8},{16,12},{20,16},{24,20},{28,24},{5,1},{9,5},{13... | collective-permute-start | bytes 737288 | tf_op jit(solution)/shard_map/ppermute | solution.py:335
  60.4 1.3 %dynamic-slice_bitcast_fusion.sweep_ref = f32[3,32]{1,0:T(4,128)} fusion(f32[8,3,32]{2,1,0:T(4,128)} %constant.87.clone, s32[]{:T(128)S(6)} %select_n.32), kind=kLoop, calls=%fused_computation.14 | loop fusion | bytes 772 | tf_op jit(solution)/shard_map/jit(dynamic_index_in_dim)/squeeze | solution.py:300
  61.7 1.2 %fusion.6.edges_ref = f32[1,24]{1,0:T(1,128)} fusion(f32[8,1,24]{2,1,0:T(1,128)} %constant.88.clone, s32[]{:T(128)S(6)} %select_n.32), kind=kLoop, calls=%fused_computation.27 | loop fusion | bytes 196 | tf_op jit(solution)/shard_map/jit(dynamic_index_in_dim)/squeeze | solution.py:300
  62.9 0.8 copy.22.along_z_ref
  63.6 0.8 copy.20
  64.4 0.8 copy.21
  65.2 0.8 pad_maximum_fusion.right_ref
  66.0 1.1 %collective-permute-done.5 = f32[5,48,256]{2,1,0:T(8,128)S(1)} collective-permute-done((f32[5,48,256]{2,1,0:T(8,128)S(1)}, f32[5,48,256]{2,1,0:T(8,128)S(1)}, u32[]{:S(2)}, u32[]{:S(2)}) %collective-permute-start.5) | collective-permute-done | bytes 245792 | tf_op jit(solution)/shard_map/ppermute | solution.py:335
  67.2 0.8 pad_maximum_fusion.1.left_ref
  68.0 0.7 copy-done
  68.9 25.9 %shard_map.132 = (f32[4,32,48,256]{3,2,1,0:T(8,128)}, f32[64,512]{1,0:T(8,128)}) custom-call(s32[1,192]{1,0:T(1,128)} %bitcast.39, f32[3,32]{1,0:T(4,128)} %dynamic-slice_bitcast_fusion.sweep_ref, f32[1,24]{1,0:T(1,128)} %fusion.6.edges_ref, f32[4,32,48,256]{3,2,1,0:T(8,128)} %state_ref.3, f32[32,48,256]{2,1,0:T(8,128)} %flow_ref.3, ...), custom_call_target="tpu_custom_call" | custom-call | tf_op jit(solution)/shard_map/pallas_call | solution.py:353
  94.8 1.0 copy.23
  96.1 11.7 %all_to_all.10 = f32[32,1,1024]{2,1,0:T(1,128)S(1)} all-to-all(f32[32,1,1024]{2,1,0:T(1,128)S(1)} %all_to_all.8), channel_id=1, replica_groups=mesh['gx'=8,'yz'=4] {'gx','yz'}, dimensions={0} | all-to-all | bytes 262144 | tf_op jit(solution)/shard_map/all_to_all | solution.py:389
  107.9 0.7 reshape.27
  (22 shorter events, 1.9 us)
Async XLA Ops:
  0.6 43.3 %copy-start.4 = (s32[192]{0:T(256)S(1)}, s32[192]{0:T(256)}, u32[]{:S(2)}) copy-start(s32[192]{0:T(256)} %param.14) | copy-start | bytes 2308
  1.9 61.7 %copy-start.2 = (f32[3,192]{1,0:T(4,128)S(1)}, f32[3,192]{1,0:T(4,128)}, u32[]{:S(2)}) copy-start(f32[3,192]{1,0:T(4,128)} %param.15) | copy-start | bytes 6916
  1.9 62.5 %copy-start.3 = (f32[3,192]{1,0:T(4,128)S(1)}, f32[3,192]{1,0:T(4,128)}, u32[]{:S(2)}) copy-start(f32[3,192]{1,0:T(4,128)} %param.16) | copy-start | bytes 6916
  8.0 27.1 %collective-permute-start = (f32[2,5,48,256]{3,2,1,0:T(8,128)}, f32[2,5,48,256]{3,2,1,0:T(8,128)S(1)}, u32[]{:S(2)}, u32[]{:S(2)}) collective-permute-start(f32[2,5,48,256]{3,2,1,0:T(8,128)} %get-tuple-element.6), channel_id=1, source_target_pairs={{0,4},{4,8},{8,12},{12,16},{16,20},{20,24},{24,28},{1,5},{5,9},{9,... | collective-permute-start | bytes 1474568 | tf_op jit(solution)/shard_map/ppermute | solution.py:329
  15.4 52.6 %collective-permute-start.6 = (f32[3,32,3,256]{3,2,1,0:T(4,128)S(1)}, f32[3,32,3,256]{3,2,1,0:T(4,128)S(1)}, u32[]{:S(2)}, u32[]{:S(2)}) collective-permute-start(f32[3,32,3,256]{3,2,1,0:T(4,128)S(1)} %pad_maximum_fusion.2), channel_id=1, source_target_pairs={{0,1},{1,2},{2,3},{4,5},{5,6},{6,7},{8,9},{9,10},{10,11},{12,13},{... | collective-permute-start | bytes 884744 | tf_op jit(solution)/shard_map/ppermute | solution.py:326
  16.9 24.1 %collective-permute-start.3 = (f32[2,5,48,256]{3,2,1,0:T(8,128)}, f32[2,5,48,256]{3,2,1,0:T(8,128)S(1)}, u32[]{:S(2)}, u32[]{:S(2)}) collective-permute-start(f32[2,5,48,256]{3,2,1,0:T(8,128)} %get-tuple-element.7), channel_id=1, source_target_pairs={{4,0},{8,4},{12,8},{16,12},{20,16},{24,20},{28,24},{5,1},{9,5},{13... | collective-permute-start | bytes 1474568 | tf_op jit(solution)/shard_map/ppermute | solution.py:330
  18.3 49.7 %collective-permute-start.7 = (f32[3,32,3,256]{3,2,1,0:T(4,128)S(1)}, f32[3,32,3,256]{3,2,1,0:T(4,128)S(1)}, u32[]{:S(2)}, u32[]{:S(2)}) collective-permute-start(f32[3,32,3,256]{3,2,1,0:T(4,128)S(1)} %pad_maximum_fusion.3), channel_id=1, source_target_pairs={{1,0},{2,1},{3,2},{5,4},{6,5},{7,6},{9,8},{10,9},{11,10},{13,12},{... | collective-permute-start | bytes 884744 | tf_op jit(solution)/shard_map/ppermute | solution.py:327
  36.7 14.8 %collective-permute-start.1 = (f32[5,48,256]{2,1,0:T(8,128)S(1)}, f32[5,48,256]{2,1,0:T(8,128)S(1)}, u32[]{:S(2)}, u32[]{:S(2)}) collective-permute-start(f32[5,48,256]{2,1,0:T(8,128)S(1)} %fusion.3), channel_id=1, source_target_pairs={{0,4},{4,8},{8,12},{12,16},{16,20},{20,24},{24,28},{1,5},{5,9},{9,... | collective-permute-start | bytes 737288 | tf_op jit(solution)/shard_map/ppermute | solution.py:334
  42.7 14.8 %collective-permute-start.4 = (f32[5,48,256]{2,1,0:T(8,128)S(1)}, f32[5,48,256]{2,1,0:T(8,128)S(1)}, u32[]{:S(2)}, u32[]{:S(2)}) collective-permute-start(f32[5,48,256]{2,1,0:T(8,128)S(1)} %fusion.1), channel_id=1, source_target_pairs={{4,0},{8,4},{12,8},{16,12},{20,16},{24,20},{28,24},{5,1},{9,5},{13... | collective-permute-start | bytes 737288 | tf_op jit(solution)/shard_map/ppermute | solution.py:335
  53.0 12.2 %collective-permute-start.2 = (f32[5,48,256]{2,1,0:T(8,128)S(1)}, f32[5,48,256]{2,1,0:T(8,128)S(1)}, u32[]{:S(2)}, u32[]{:S(2)}) collective-permute-start(f32[5,48,256]{2,1,0:T(8,128)S(1)} %bitcast_add_fusion.1), channel_id=1, source_target_pairs={{0,4},{4,8},{8,12},{12,16},{16,20},{20,24},{24,28},{1,5},{5,9},{9,... | collective-permute-start | bytes 737288 | tf_op jit(solution)/shard_map/ppermute | solution.py:334
  59.1 8.1 %collective-permute-start.5 = (f32[5,48,256]{2,1,0:T(8,128)S(1)}, f32[5,48,256]{2,1,0:T(8,128)S(1)}, u32[]{:S(2)}, u32[]{:S(2)}) collective-permute-start(f32[5,48,256]{2,1,0:T(8,128)S(1)} %bitcast_add_fusion), channel_id=1, source_target_pairs={{4,0},{8,4},{12,8},{16,12},{20,16},{24,20},{28,24},{5,1},{9,5},{13... | collective-permute-start | bytes 737288 | tf_op jit(solution)/shard_map/ppermute | solution.py:335
  68.0 0.8 copy-start
  68.0 0.9 copy-start.1

commit v2 on v1

--- a/solution.py
+++ b/solution.py
@@ -88,9 +88,7 @@
             if e - 2 + k < count:
                 taps[d, 2, k + 2] = rows[e - 2, e - 2 + k]
         ends[d, 0] = -1.0 / down[s + 1]
-        ends[d, 1] = taps[d, 1, 1] / down[s + 1] if d > 0 else 0.0
         ends[d, 2] = -1.0 / up[e - 2]
-        ends[d, 3] = taps[d, 2, 3] / up[e - 2] if d < blocks - 1 else 0.0
         if d > 0:
             ends[d, 1] = rows[s + 1, s - 1] / down[s + 1]
         if d < blocks - 1:
@@ -108,27 +106,158 @@
     )
 
 
-def sums_kernel(cells, weights_ref, state_ref, flow_ref, right_ref, left_ref):
-    def load(f, i):
-        return flow_ref[i] if f == 4 else state_ref[f, i]
-
-    for f in range(5):
-        total_right = weights_ref[0, 0] * load(f, 0)
-        total_left = weights_ref[1, 0] * load(f, 0)
-        for i in range(1, cells):
-            value = load(f, i)
-            total_right += weights_ref[0, i] * value
-            total_left += weights_ref[1, i] * value
-        right_ref[0, f] = total_right
-        left_ref[0, f] = total_left
-        right_ref[1, f] = load(f, cells - 1)
-        left_ref[1, f] = load(f, 0)
+def exchange_kernel(
+    sizes, weights_ref, chain_ref, state_ref, flow_ref,
+    left_sum, left_plane, right_sum, right_plane, low_ref, high_ref,
+    field, to_right, to_left, on_right, on_left, far_left, far_right,
+    load_sem, send_sem, recv_sem,
+):
+    blocks, groups = sizes
+    _, cells, width, _ = field.shape
+    block, group = lax.axis_index("gx"), lax.axis_index("yz")
+    order = (0, 2, 4, 1, 3)
+    crossing = (0, 2, 4)
+    shifts = {"gx": (1, -1, 2, -2), "yz": (1, -1)}
+    place = {"gx": (block, blocks), "yz": (group, groups)}
+
+    def there(axis, shift):
+        index, count = place[axis]
+        return index + shift < count if shift > 0 else index + shift >= 0
+
+    def other(axis, shift):
+        index, count = place[axis]
+        return {axis: jnp.clip(index + shift, 0, count - 1)}
+
+    loads = {}
+    for f in order:
+        source = flow_ref if f == 4 else state_ref.at[f]
+        loads[f] = pltpu.make_async_copy(source, field.at[f], load_sem.at[f])
+        loads[f].start()
+
+    barrier = pltpu.get_barrier_semaphore()
+    pairs = [(axis, shift) for axis in shifts for shift in shifts[axis]]
+    for axis, shift in pairs:
+        @pl.when(there(axis, shift))
+        def _():
+            pl.semaphore_signal(
+                barrier, inc=1, device_id=other(axis, shift),
+                device_id_type=pl.DeviceIdType.MESH,
+            )
+    present = [there(axis, shift).astype(jnp.int32) for axis, shift in pairs]
+    pl.semaphore_wait(barrier, sum(present[1:], present[0]))
+
+    sent = []
+
+    def copy(kind, f, source, target, axis, shift):
+        moved = pltpu.make_async_remote_copy(
+            src_ref=source, dst_ref=target,
+            send_sem=send_sem.at[kind, f], recv_sem=recv_sem.at[kind, f],
+            device_id=other(axis, shift), device_id_type=pl.DeviceIdType.MESH,
+        )
+        sent.append((moved, axis, shift))
+
+        @pl.when(there(axis, shift))
+        def _():
+            moved.start()
+
+        return moved, axis, shift
+
+    def arrive(entry, targets):
+        moved, axis, shift = entry
+
+        @pl.when(there(axis, -shift))
+        def _():
+            moved.wait_recv()
+
+        @pl.when(jnp.logical_not(there(axis, -shift)))
+        def _():
+            targets[...] = jnp.zeros_like(targets)
+
+    near, rest = {}, []
+    for f in order:
+        loads[f].wait()
+        plane_r = copy(0, f, field.at[f, cells - 1], left_plane.at[f], "gx", 1)
+        plane_l = copy(1, f, field.at[f, 0], right_plane.at[f], "gx", -1)
+        rest += [(plane_r, left_plane.at[f]), (plane_l, right_plane.at[f])]
+        if f in crossing:
+            slot = crossing.index(f)
+            rest.append((copy(
+                2, f, field.at[f, :, width - TILE:width], low_ref.at[slot], "yz", 1
+            ), low_ref.at[slot]))
+            rest.append((copy(
+                3, f, field.at[f, :, 0:TILE], high_ref.at[slot], "yz", -1
+            ), high_ref.at[slot]))
+        for j in range(0, width, TILE):
+            total_right = weights_ref[0, 0] * field[f, 0, j:j + TILE]
+            total_left = weights_ref[1, 0] * field[f, 0, j:j + TILE]
+            for i in range(1, cells):
+                value = field[f, i, j:j + TILE]
+                total_right += weights_ref[0, i] * value
+                total_left += weights_ref[1, i] * value
+            to_right[f, j:j + TILE] = total_right
+            to_left[f, j:j + TILE] = total_left
+        near[f] = (
+            copy(4, f, to_right.at[f], left_sum.at[f], "gx", 1),
+            copy(5, f, to_left.at[f], right_sum.at[f], "gx", -1),
+        )
+    far = {}
+    for f in order:
+        arrive(near[f][0], left_sum.at[f])
+        arrive(near[f][1], right_sum.at[f])
+        on_right[f] = to_right[f] + chain_ref[0, 0] * left_sum[f]
+        on_left[f] = to_left[f] + chain_ref[0, 1] * right_sum[f]
+        far[f] = (
+            copy(6, f, on_right.at[f], far_left.at[f], "gx", 2),
+            copy(7, f, on_left.at[f], far_right.at[f], "gx", -2),
+        )
+    for f in order:
+        arrive(far[f][0], far_left.at[f])
+        arrive(far[f][1], far_right.at[f])
+    for entry, targets in rest:
+        arrive(entry, targets)
+    for moved, axis, shift in sent:
+        @pl.when(there(axis, shift))
+        def _():
+            moved.wait_send()
+    for f in order:
+        left_sum[f] = left_sum[f] + chain_ref[0, 2] * far_left[f]
+        right_sum[f] = right_sum[f] + chain_ref[0, 3] * far_right[f]
+
+
+def signal_kernel(groups, count, piece_ref, out_ref, landing, send_sem, recv_sem):
+    me = lax.axis_index("gx") * groups + lax.axis_index("yz")
+
+    def partner(k):
+        index = lax.rem(me + k, count)
+        return {"gx": lax.div(index, groups), "yz": lax.rem(index, groups)}, index
+
+    barrier = pltpu.get_barrier_semaphore()
+    for k in range(1, count):
+        pl.semaphore_signal(
+            barrier, inc=1, device_id=partner(k)[0], device_id_type=pl.DeviceIdType.MESH
+        )
+    pl.semaphore_wait(barrier, count - 1)
+    copies = []
+    for k in range(1, count):
+        target, index = partner(k)
+        copies.append(pltpu.make_async_remote_copy(
+            src_ref=piece_ref.at[index], dst_ref=landing.at[k - 1],
+            send_sem=send_sem.at[k - 1], recv_sem=recv_sem.at[k - 1],
+            device_id=target, device_id_type=pl.DeviceIdType.MESH,
+        ))
+        copies[-1].start()
+    for moved in copies:
+        moved.wait()
+    total = piece_ref[me]
+    for k in range(count - 1):
+        total += landing[k]
+    out_ref[...] = total
 
 
 def main_kernel(
     cells, width, depth,
     row_ref, sweep_ref, edges_ref,
-    state_ref, flow_ref, right_ref, left_ref, low_ref, high_ref,
+    state_ref, flow_ref, left_sum, left_plane, right_sum, right_plane, low_ref, high_ref,
     zhi_ref, zlo_ref, along_z_ref, normal_ref, pos_ref, observer_ref, bin_ref,
     next_ref, signal_ref,
     wide, swept, zrate, rate, picked,
@@ -146,8 +275,8 @@
             for slot, f in enumerate((0, 2, 4)):
                 body = flow_ref[i] if f == 4 else state_ref[f, i]
                 wide[slot, i, TILE:TILE + width, :] = body
-                wide[slot, i, TILE - 3:TILE, :] = low_ref[slot, i]
-                wide[slot, i, TILE + width:TILE + width + 3, :] = high_ref[slot, i]
+                wide[slot, i, 0:TILE, :] = low_ref[slot, i]
+                wide[slot, i, TILE + width:2 * TILE + width, :] = high_ref[slot, i]
             return carry
         lax.fori_loop(0, cells, widen, 0)
 
@@ -172,11 +301,11 @@
     carry = []
     for f in fields:
         first = tap(0, 0) * load(f, 0) + tap(0, 1) * load(f, 1) + tap(0, 2) * load(f, 2)
-        value = first + end(0) * right_ref[0, f] + end(1) * right_ref[1, f]
+        value = first + end(0) * left_sum[f] + end(1) * left_plane[f]
         swept[f, 0] = value
         second = (
             tap(1, -1) * load(f, 0) + tap(1, 0) * load(f, 1)
-            + tap(1, 1) * load(f, 2) + tap(1, 2) * load(f, 3) + tap(1, -2) * right_ref[1, f]
+            + tap(1, 1) * load(f, 2) + tap(1, 2) * load(f, 3) + tap(1, -2) * left_plane[f]
         )
         value = second - sweep_ref[0, 1] * value
         swept[f, 1] = value
@@ -200,13 +329,13 @@
     for f in fields:
         before = (
             tap(2, -2) * load(f, n - 4) + tap(2, -1) * load(f, n - 3) + tap(2, 0) * load(f, n - 2)
-            + tap(2, 1) * load(f, n - 1) + tap(2, 2) * left_ref[1, f]
+            + tap(2, 1) * load(f, n - 1) + tap(2, 2) * right_plane[f]
         )
         value = before - sweep_ref[0, n - 2] * carry[f]
         swept[f, n - 2] = value
         last = (
             tap(3, -2) * load(f, n - 3) + tap(3, -1) * load(f, n - 2) + tap(3, 0) * load(f, n - 1)
-            + end(2) * left_ref[0, f] + end(3) * left_ref[1, f]
+            + end(2) * right_sum[f] + end(3) * right_plane[f]
         )
         solved.append((last - sweep_ref[0, n - 1] * value) * sweep_ref[1, n - 1])
 
@@ -300,41 +429,36 @@
         return lax.dynamic_index_in_dim(jnp.asarray(table), block, 0, keepdims=False)
 
     params = dict(vmem_limit_bytes=60 * 1024 * 1024)
-    plane = jax.ShapeDtypeStruct((2, 5, width, depth), jnp.float32)
-    plane_spec = pl.BlockSpec((2, 5, TILE, depth), lambda j: (0, 0, j, 0))
-    to_right, to_left = pl.pallas_call(
-        functools.partial(sums_kernel, cells),
-        grid=(tiles,),
-        out_shape=(plane, plane),
+    assert hops <= 3
+    links = np.zeros((blocks, 1, 4), np.float32)
+    links[:, 0, :2] = chain
+    links[1:, 0, 2] = chain[:-1, 0]
+    links[:-1, 0, 3] = chain[1:, 1]
+    plane = jax.ShapeDtypeStruct((5, width, depth), jnp.float32)
+    edge = jax.ShapeDtypeStruct((3, cells, TILE, depth), jnp.float32)
+    plane_spec = pl.BlockSpec((5, TILE, depth), lambda j: (0, j, 0))
+    scratch_plane = VMEM((5, width, depth), jnp.float32)
+    received = pl.pallas_call(
+        functools.partial(exchange_kernel, sizes),
+        out_shape=(plane,) * 4 + (edge,) * 2,
         in_specs=[
             pl.BlockSpec(memory_space=SMEM),
-            pl.BlockSpec((4, cells, TILE, depth), lambda j: (0, 0, j, 0)),
-            pl.BlockSpec((cells, TILE, depth), lambda j: (0, j, 0)),
+            pl.BlockSpec(memory_space=SMEM),
+            pl.BlockSpec(memory_space=pl.ANY),
+            pl.BlockSpec(memory_space=pl.ANY),
         ],
-        out_specs=(plane_spec, plane_spec),
-        compiler_params=pltpu.CompilerParams(**params),
-    )(mine(weights), state, mean_flow)
-
-    def neighbours(count):
-        up = [(i, i + 1) for i in range(count - 1)]
-        return up, [(b, a) for a, b in up]
-
-    up, down = neighbours(groups)
-    crossing = lambda a, b: jnp.stack(
-        [state[0, :, a:b], state[2, :, a:b], mean_flow[:, a:b]]
-    )
-    low = lax.ppermute(crossing(width - 3, width), "yz", up)
-    high = lax.ppermute(crossing(0, 3), "yz", down)
-    up, down = neighbours(blocks)
-    from_left = lax.ppermute(to_right, "gx", up)
-    from_right = lax.ppermute(to_left, "gx", down)
-    own = mine(chain)
-    sum_left, sum_right = from_left[0], from_right[0]
-    for _ in range(hops - 1):
-        sum_left = lax.ppermute(to_right[0] + own[0] * sum_left, "gx", up)
-        sum_right = lax.ppermute(to_left[0] + own[1] * sum_right, "gx", down)
-    from_left = jnp.stack([sum_left, from_left[1]])
-    from_right = jnp.stack([sum_right, from_right[1]])
+        out_specs=(pl.BlockSpec(memory_space=VMEM),) * 6,
+        scratch_shapes=[VMEM((5, cells, width, depth), jnp.float32)]
+        + [scratch_plane] * 6
+        + [
+            pltpu.SemaphoreType.DMA((5,)),
+            pltpu.SemaphoreType.DMA((8, 5)),
+            pltpu.SemaphoreType.DMA((8, 5)),
+        ],
+        compiler_params=pltpu.CompilerParams(
+            collective_id=0, has_side_effects=True, vmem_limit_bytes=40 * 1024 * 1024
+        ),
+    )(mine(weights), mine(links), state, mean_flow)
 
     operator = dense_derivative(depth).T.astype(np.float32)
     z_high = jnp.asarray(operator).astype(jnp.bfloat16)
@@ -360,8 +484,8 @@
         in_specs=[
             smem, smem, smem,
             whole(4, cells, width, depth), whole(cells, width, depth),
-            plane_spec, plane_spec,
-            whole(3, cells, 3, depth), whole(3, cells, 3, depth),
+            plane_spec, plane_spec, plane_spec, plane_spec,
+            whole(3, cells, TILE, depth), whole(3, cells, TILE, depth),
             whole(depth, depth), whole(depth, depth),
             whole(faces, 1), whole(faces, 3), whole(faces, 3),
             whole(3, observers), whole(faces, observers),
@@ -380,14 +504,24 @@
         compiler_params=pltpu.CompilerParams(**params),
     )(
         row, mine(sweep), mine(edges.reshape(blocks, 1, -1)),
-        state, mean_flow, from_left, from_right, low, high,
+        state, mean_flow, *received,
         z_high, z_low, along_z.reshape(faces, 1), face_normal.T, face_pos.T,
         observer_pos, time_bin,
     )
     devices = blocks * groups
-    pieces = signal.T.reshape(devices, -1)
-    pieces = lax.all_to_all(pieces, ("gx", "yz"), split_axis=0, concat_axis=0, tiled=True)
-    signal = jnp.sum(pieces.reshape(devices, -1), axis=0).reshape(observers // devices, BINS)
+    share = observers // devices
+    signal = pl.pallas_call(
+        functools.partial(signal_kernel, groups, devices),
+        out_shape=jax.ShapeDtypeStruct((share, BINS), jnp.float32),
+        in_specs=[pl.BlockSpec(memory_space=VMEM)],
+        out_specs=pl.BlockSpec(memory_space=VMEM),
+        scratch_shapes=[
+            VMEM((devices - 1, share, BINS), jnp.float32),
+            pltpu.SemaphoreType.DMA((devices - 1,)),
+            pltpu.SemaphoreType.DMA((devices - 1,)),
+        ],
+        compiler_params=pltpu.CompilerParams(collective_id=1, has_side_effects=True),
+    )(signal.T.reshape(devices, share, BINS))
     return state_next, signal
 
 

time: 109 us -> 90.9 us (0.83)
  Pallas kernels: 32 us -> 68.8 us
  waiting for transfers between devices: 22.4 us -> 0 us
  starting transfers between devices: 20.2 us -> 0 us
  blocking collectives: 11.7 us -> 0 us
  other arithmetic: 8.84 us -> 1.24 us
  local copies, waits for them, and re-layouts: 12.5 us -> 19.3 us
    pallas_call x1 -> x2, Pallas kernels: 6.13 us -> 42.5 us  [the longest x1 32.2 us: per_device(): pl.pallas_call(functools.partial(exchange_kernel, sizes), out_shape=(plan...]
    ppermute x8 -> x0, waiting for transfers between devices: 22.4 us -> none  [the longest x1 14.3 us: per_device(): from_left = lax.ppermute(to_right, 'gx', up)]
    ppermute x8 -> x0, starting transfers between devices: 20.2 us -> none  [the longest x2 8.7 us: per_device(): sum_left = lax.ppermute(to_right[0] + own[0] * sum_left, 'gx', up)]
    all_to_all x1 -> x0, blocking collectives: 11.7 us -> none  [per_device(): lax.all_to_all(pieces, ('gx', 'yz'), split_axis=0, concat_axis=0, tiled=T...]
    unnamed x12 -> x19, local copies, waits for them, and re-layouts: 2.44 us -> 13 us
    add x4 -> x0, other arithmetic: 6.32 us -> none  [the longest x2 3.26 us: per_device(): sum_right = lax.ppermute(to_left[0] + own[1] * sum_right, 'gx', down)]
    slice x4 -> x0, local copies, waits for them, and re-layouts: 1.91 us -> none  [the longest x1 1.29 us: per_device(): state[0, :, a:b]]
    another operation x4 -> x0, other arithmetic: 1.84 us -> none  [the longest x1 0.83 us: per_device(): from_left = jnp.stack([sum_left, from_left[1]])]
  transfers between devices with their start and end apart: 8 -> 0, of which waited for: 3 -> 0; matrix products, arithmetic and copies ran while one was open for 16% -> 0% of each run, Pallas kernels for 0% -> 0%
where the time goes in v2:
time: 90.9 us; the launch traced here: 90 us
  Pallas kernels  68.8 us (76%)
  local copies, waits for them, and re-layouts  19.3 us (21%)
  other arithmetic  1.24 us (1%)
    pallas_call x1, Pallas kernels, per_device(): pl.pallas_call(functools.partial(exchange_kernel, sizes), out_shape=(plan...  32.2 us
    pallas_call x1, Pallas kernels, per_device(): pl.pallas_call(functools.partial(main_kernel, cells, width, depth), grid=...  26.3 us
    unnamed x19, local copies, waits for them, and re-layouts  13 us
    pallas_call x1, Pallas kernels, per_device(): pl.pallas_call(functools.partial(signal_kernel, groups, devices), out_sha...  10.3 us
    squeeze x4, local copies, waits for them, and re-layouts, mine(): lax.dynamic_index_in_dim(jnp.asarray(table), block, 0, keepdims=False)  3.85 us

profile of v2, /device:TPU:0, one launch (start us, length us, event | category | flops | bytes accessed | tf_op | source)
XLA Modules:
  0.0 90.0 jit_solution(8980272920316500815)
XLA Ops:
  0.6 0.7 fusion.3.chain_ref
  1.3 1.2 %fusion.2.edges_ref = f32[1,24]{1,0:T(1,128)} fusion(f32[8,1,24]{2,1,0:T(1,128)} %constant.86.clone, s32[]{:T(128)S(6)} %select_n.32), kind=kLoop, calls=%fused_computation.13 | loop fusion | bytes 196 | tf_op jit(solution)/shard_map/jit(dynamic_index_in_dim)/squeeze | solution.py:429
  2.5 0.7 dynamic-slice_bitcast_fusion.1.weights_ref
  3.2 1.2 %and_select_fusion = (s32[192]{0:T(256)S(1)}, s32[192]{0:T(256)}) fusion(s32[192]{0:T(256)} %param.14, s32[]{:T(128)S(6)} %mul.15, s32[]{:T(128)S(6)} %mul.12), kind=kLoop, calls=%fused_computation.1 | loop fusion | flops 6720 | bytes 2312 | tf_op jit(solution)/shard_map/jit(remainder)/select_n | solution.py:470
  4.5 1.3 %dynamic-slice_bitcast_fusion.sweep_ref = f32[3,32]{1,0:T(4,128)} fusion(f32[8,3,32]{2,1,0:T(4,128)} %constant.85.clone, s32[]{:T(128)S(6)} %select_n.32), kind=kLoop, calls=%fused_computation | loop fusion | bytes 772 | tf_op jit(solution)/shard_map/jit(dynamic_index_in_dim)/squeeze | solution.py:429
  5.7 0.8 copy.19.along_z_ref
  6.5 1.4 %copy.17 = f32[3,192]{0,1:T(8,128)} copy(f32[3,192]{1,0:T(4,128)} %param.15) | data formatting | bytes 4608 | tf_op args[3]
  7.9 1.5 %copy.18 = f32[3,192]{0,1:T(8,128)} copy(f32[3,192]{1,0:T(4,128)} %param.16) | data formatting | bytes 4608 | tf_op args[4]
  9.4 0.0 copy-start
  9.4 2.8 %copy-done = f32[4,32,48,256]{3,2,1,0:T(8,128)S(1)} copy-done((f32[4,32,48,256]{3,2,1,0:T(8,128)S(1)}, f32[4,32,48,256]{3,2,1,0:T(8,128)}, u32[]{:S(2)}) %copy-start) | copy-done | bytes 6291480
  12.2 0.0 copy-start.1
  12.2 1.4 %copy-done.1 = f32[32,48,256]{2,1,0:T(8,128)S(1)} copy-done((f32[32,48,256]{2,1,0:T(8,128)S(1)}, f32[32,48,256]{2,1,0:T(8,128)}, u32[]{:S(2)}) %copy-start.1) | copy-done | bytes 1572888
  13.6 32.2 %shard_map.131 = (f32[5,48,256]{2,1,0:T(8,128)S(1)}, f32[5,48,256]{2,1,0:T(8,128)S(1)}, f32[5,48,256]{2,1,0:T(8,128)S(1)}, f32[5,48,256]{2,1,0:T(8,128)S(1)}, f3...) custom-call(f32[2,32]{1,0:T(2,128)S(1)} %dynamic-slice_bitcast_fusion.1.weights_ref, ...), custom_call_target="tpu_custom_call" | custom-call | tf_op jit(solution)/shard_map/pallas_call | solution.py:441
  45.7 0.0 copy-start.2
  45.8 0.9 copy-done.2
  46.6 0.0 copy-start.3
  46.6 0.9 %copy-done.3 = f32[3,32,8,256]{3,2,1,0:T(8,128)} copy-done((f32[3,32,8,256]{3,2,1,0:T(8,128)}, f32[3,32,8,256]{3,2,1,0:T(8,128)S(1)}, u32[]{:S(2)}) %copy-start.3) | copy-done | bytes 786456
  47.5 0.0 copy-start.4
  47.5 0.7 copy-done.4
  48.2 0.0 copy-start.5
  48.2 0.7 copy-done.5
  48.9 0.0 copy-start.6
  48.9 0.7 copy-done.6
  49.6 0.0 copy-start.7
  49.6 0.7 copy-done.7
  50.3 26.3 %shard_map.132 = (f32[4,32,48,256]{3,2,1,0:T(8,128)}, f32[64,512]{1,0:T(8,128)}) custom-call(s32[1,192]{1,0:T(1,128)} %bitcast.18, f32[3,32]{1,0:T(4,128)} %dynamic-slice_bitcast_fusion.sweep_ref, f32[1,24]{1,0:T(1,128)} %fusion.2.edges_ref, f32[4,32,48,256]{3,2,1,0:T(8,128)} %state_ref.3, f32[32,48,256]{2,1,0:T(8,128)} %flow_ref.3, ...), custom_call_target="tpu_custom_call" | custom-call | tf_op jit(solution)/shard_map/pallas_call | solution.py:477
  76.6 1.7 %copy.20 = f32[512,64]{1,0:T(8,128)} copy(f32[512,64]{0,1:T(8,128)} %bitcast.17) | data formatting | bytes 262144 | tf_op jit(solution)/shard_map/transpose | solution.py:524
  78.4 10.3 %shard_map.133 = f32[16,64]{1,0:T(8,128)} custom-call(f32[32,16,64]{2,1,0:T(8,128)} %bitcast.14), custom_call_target="tpu_custom_call" | custom-call | tf_op jit(solution)/shard_map/pallas_call | solution.py:513
  88.7 1.3 %copy.22 = f32[16,64]{1,0:T(8,128)} copy(f32[16,64]{1,0:T(8,128)} %shard_map.133) | data formatting | bytes 8192
Async XLA Ops:
  9.4 2.8 %copy-start = (f32[4,32,48,256]{3,2,1,0:T(8,128)S(1)}, f32[4,32,48,256]{3,2,1,0:T(8,128)}, u32[]{:S(2)}) copy-start(f32[4,32,48,256]{3,2,1,0:T(8,128)} %state_ref.3) | copy-start | bytes 18874372
  12.2 1.4 %copy-start.1 = (f32[32,48,256]{2,1,0:T(8,128)S(1)}, f32[32,48,256]{2,1,0:T(8,128)}, u32[]{:S(2)}) copy-start(f32[32,48,256]{2,1,0:T(8,128)} %flow_ref.3) | copy-start | bytes 4718596
  45.7 0.9 copy-start.2
  46.6 0.9 %copy-start.3 = (f32[3,32,8,256]{3,2,1,0:T(8,128)}, f32[3,32,8,256]{3,2,1,0:T(8,128)S(1)}, u32[]{:S(2)}) copy-start(f32[3,32,8,256]{3,2,1,0:T(8,128)S(1)} %get-tuple-element.15.high_ref) | copy-start | bytes 2359300
  47.5 0.7 copy-start.4
  48.2 0.7 copy-start.5
  48.9 0.7 copy-start.6
  49.6 0.7 copy-start.7

commit v3 on v2

--- a/solution.py
+++ b/solution.py
@@ -107,16 +107,20 @@
 
 
 def exchange_kernel(
-    sizes, weights_ref, chain_ref, state_ref, flow_ref,
-    left_sum, left_plane, right_sum, right_plane, low_ref, high_ref,
-    field, to_right, to_left, on_right, on_left, far_left, far_right,
-    load_sem, send_sem, recv_sem,
+    sizes, table_ref, state_ref, flow_ref, zhi_ref, zlo_ref,
+    left_sum, left_plane, right_sum, right_plane, low_ref, high_ref, z_out,
+    zrate, field, to_right, to_left, on_right, on_left, far_left, far_right,
+    load_sem, store_sem, send_sem, recv_sem,
 ):
     blocks, groups = sizes
     _, cells, width, _ = field.shape
     block, group = lax.axis_index("gx"), lax.axis_index("yz")
     order = (0, 2, 4, 1, 3)
     crossing = (0, 2, 4)
+
+    def weight(side, i):
+        return table_ref[0, side * cells + i]
+
     shifts = {"gx": (1, -1, 2, -2), "yz": (1, -1)}
     place = {"gx": (block, blocks), "yz": (group, groups)}
 
@@ -188,24 +192,42 @@
                 3, f, field.at[f, :, 0:TILE], high_ref.at[slot], "yz", -1
             ), high_ref.at[slot]))
         for j in range(0, width, TILE):
-            total_right = weights_ref[0, 0] * field[f, 0, j:j + TILE]
-            total_left = weights_ref[1, 0] * field[f, 0, j:j + TILE]
+            total_right = weight(0, 0) * field[f, 0, j:j + TILE]
+            total_left = weight(1, 0) * field[f, 0, j:j + TILE]
             for i in range(1, cells):
                 value = field[f, i, j:j + TILE]
-                total_right += weights_ref[0, i] * value
-                total_left += weights_ref[1, i] * value
+                total_right += weight(0, i) * value
+                total_left += weight(1, i) * value
             to_right[f, j:j + TILE] = total_right
             to_left[f, j:j + TILE] = total_left
         near[f] = (
             copy(4, f, to_right.at[f], left_sum.at[f], "gx", 1),
             copy(5, f, to_left.at[f], right_sum.at[f], "gx", -1),
         )
+    stores = []
+    group_of = 4 if cells % 4 == 0 else 1
+    for slot, f in enumerate((0, 3, 4)):
+        def multiply(k, carry, slot=slot, f=f):
+            planes = pl.ds(k * group_of, group_of)
+            block = field[f, planes].reshape(group_of * width, -1)
+            high = block.astype(jnp.bfloat16)
+            rest = (block - high.astype(jnp.float32)).astype(jnp.bfloat16)
+            out = jnp.dot(rest, zhi_ref[...], preferred_element_type=jnp.float32)
+            out += jnp.dot(high, zlo_ref[...], preferred_element_type=jnp.float32)
+            out += jnp.dot(high, zhi_ref[...], preferred_element_type=jnp.float32)
+            zrate[slot, planes] = out.reshape(group_of, width, -1)
+            return carry
+        lax.fori_loop(0, cells // group_of, multiply, 0)
+        stores.append(pltpu.make_async_copy(
+            zrate.at[slot], z_out.at[slot], store_sem.at[slot]
+        ))
+        stores[-1].start()
     far = {}
     for f in order:
         arrive(near[f][0], left_sum.at[f])
         arrive(near[f][1], right_sum.at[f])
-        on_right[f] = to_right[f] + chain_ref[0, 0] * left_sum[f]
-        on_left[f] = to_left[f] + chain_ref[0, 1] * right_sum[f]
+        on_right[f] = to_right[f] + table_ref[0, 5 * cells + 0] * left_sum[f]
+        on_left[f] = to_left[f] + table_ref[0, 5 * cells + 1] * right_sum[f]
         far[f] = (
             copy(6, f, on_right.at[f], far_left.at[f], "gx", 2),
             copy(7, f, on_left.at[f], far_right.at[f], "gx", -2),
@@ -215,13 +237,15 @@
         arrive(far[f][1], far_right.at[f])
     for entry, targets in rest:
         arrive(entry, targets)
+    for store in stores:
+        store.wait()
     for moved, axis, shift in sent:
         @pl.when(there(axis, shift))
         def _():
             moved.wait_send()
     for f in order:
-        left_sum[f] = left_sum[f] + chain_ref[0, 2] * far_left[f]
-        right_sum[f] = right_sum[f] + chain_ref[0, 3] * far_right[f]
+        left_sum[f] = left_sum[f] + table_ref[0, 5 * cells + 2] * far_left[f]
+        right_sum[f] = right_sum[f] + table_ref[0, 5 * cells + 3] * far_right[f]
 
 
 def signal_kernel(groups, count, piece_ref, out_ref, landing, send_sem, recv_sem):
@@ -256,11 +280,11 @@
 
 def main_kernel(
     cells, width, depth,
-    row_ref, sweep_ref, edges_ref,
+    row_ref, table_ref,
     state_ref, flow_ref, left_sum, left_plane, right_sum, right_plane, low_ref, high_ref,
-    zhi_ref, zlo_ref, along_z_ref, normal_ref, pos_ref, observer_ref, bin_ref,
+    zrate, geometry_ref, observer_ref, bin_ref,
     next_ref, signal_ref,
-    wide, swept, zrate, rate, picked,
+    wide, swept, rate, picked,
 ):
     step = pl.program_id(0)
     rows = pl.ds(pl.multiple_of(step * TILE, TILE), TILE)
@@ -280,23 +304,16 @@
             return carry
         lax.fori_loop(0, cells, widen, 0)
 
-    for slot, f in enumerate((0, 3, 4)):
-        block = flow_ref[:, rows, :] if f == 4 else state_ref[f, :, rows, :]
-        block = block.reshape(cells * TILE, depth)
-        high = block.astype(jnp.bfloat16)
-        rest = (block - high.astype(jnp.float32)).astype(jnp.bfloat16)
-        out = jnp.dot(rest, zhi_ref[...], preferred_element_type=jnp.float32)
-        out += jnp.dot(high, zlo_ref[...], preferred_element_type=jnp.float32)
-        out += jnp.dot(high, zhi_ref[...], preferred_element_type=jnp.float32)
-        zrate[slot] = out.reshape(cells, TILE, depth)
-
     fields = range(5)
 
     def tap(k, position):
-        return edges_ref[0, k * TAPS + position + 2]
+        return table_ref[0, 5 * cells + 4 + k * TAPS + position + 2]
 
     def end(k):
-        return edges_ref[0, 4 * TAPS + k]
+        return table_ref[0, 5 * cells + 4 + 4 * TAPS + k]
+
+    def sweep(k, i):
+        return table_ref[0, (2 + k) * cells + i]
 
     carry = []
     for f in fields:
@@ -307,13 +324,13 @@
             tap(1, -1) * load(f, 0) + tap(1, 0) * load(f, 1)
             + tap(1, 1) * load(f, 2) + tap(1, 2) * load(f, 3) + tap(1, -2) * left_plane[f]
         )
-        value = second - sweep_ref[0, 1] * value
+        value = second - sweep(0, 1) * value
         swept[f, 1] = value
         carry.append(value)
 
     def forward(i, carry):
         new = []
-        factor = sweep_ref[0, i]
+        factor = sweep(0, i)
         for f in fields:
             rhs = 7.0 / 9.0 * (load(f, i + 1) - load(f, i - 1)) + 1.0 / 36.0 * (
                 load(f, i + 2) - load(f, i - 2)
@@ -331,13 +348,13 @@
             tap(2, -2) * load(f, n - 4) + tap(2, -1) * load(f, n - 3) + tap(2, 0) * load(f, n - 2)
             + tap(2, 1) * load(f, n - 1) + tap(2, 2) * right_plane[f]
         )
-        value = before - sweep_ref[0, n - 2] * carry[f]
+        value = before - sweep(0, n - 2) * carry[f]
         swept[f, n - 2] = value
         last = (
             tap(3, -2) * load(f, n - 3) + tap(3, -1) * load(f, n - 2) + tap(3, 0) * load(f, n - 1)
             + end(2) * right_sum[f] + end(3) * right_plane[f]
         )
-        solved.append((last - sweep_ref[0, n - 1] * value) * sweep_ref[1, n - 1])
+        solved.append((last - sweep(0, n - 1) * value) * sweep(1, n - 1))
 
     def y_rate(slot, i):
         whole = wide[slot, i, window, :]
@@ -372,7 +389,7 @@
     def backward(k, carry):
         i = n - 2 - k
         x = tuple(
-            swept[f, i] * sweep_ref[1, i] - sweep_ref[2, i] * carry[f] for f in fields
+            swept[f, i] * sweep(1, i) - sweep(2, i) * carry[f] for f in fields
         )
         finish(i, x)
         return x
@@ -390,13 +407,13 @@
             return carry
 
         lax.fori_loop(0, faces, pick, 0, unroll=4)
-        mask = lax.broadcasted_iota(jnp.int32, (faces, depth), 1) == along_z_ref[...]
+        mask = lax.broadcasted_iota(jnp.int32, (faces, depth), 1) == geometry_ref[:, 6:7].astype(jnp.int32)
         at = [
             jnp.sum(jnp.where(mask, picked[c], 0.0), axis=1, keepdims=True) for c in range(5)
         ]
-        normal = [normal_ref[:, c:c + 1] for c in range(3)]
+        normal = [geometry_ref[:, c:c + 1] for c in range(3)]
         normal_rate = normal[0] * at[1] + normal[1] * at[2] + normal[2] * at[3]
-        offset = [observer_ref[c:c + 1, :] - pos_ref[:, c:c + 1] for c in range(3)]
+        offset = [observer_ref[c:c + 1, :] - geometry_ref[:, 3 + c:4 + c] for c in range(3)]
         distance = jnp.sqrt(
             offset[0] * offset[0] + offset[1] * offset[1] + offset[2] * offset[2]
         )
@@ -425,50 +442,59 @@
     block, group = lax.axis_index("gx"), lax.axis_index("yz")
     weights, chain, sweep, edges, hops = x_tables(blocks, cells)
 
-    def mine(table):
-        return lax.dynamic_index_in_dim(jnp.asarray(table), block, 0, keepdims=False)
-
     params = dict(vmem_limit_bytes=60 * 1024 * 1024)
     assert hops <= 3
     links = np.zeros((blocks, 1, 4), np.float32)
     links[:, 0, :2] = chain
     links[1:, 0, 2] = chain[:-1, 0]
     links[:-1, 0, 3] = chain[1:, 1]
+    tables = np.concatenate(
+        [part.reshape(blocks, 1, -1) for part in (weights, sweep, links, edges)], axis=2
+    )
+    table = lax.dynamic_index_in_dim(jnp.asarray(tables), block, 0, keepdims=False)
     plane = jax.ShapeDtypeStruct((5, width, depth), jnp.float32)
     edge = jax.ShapeDtypeStruct((3, cells, TILE, depth), jnp.float32)
     plane_spec = pl.BlockSpec((5, TILE, depth), lambda j: (0, j, 0))
     scratch_plane = VMEM((5, width, depth), jnp.float32)
-    received = pl.pallas_call(
+    operator = dense_derivative(depth).T.astype(np.float32)
+    z_high = jnp.asarray(operator).astype(jnp.bfloat16)
+    z_low = (jnp.asarray(operator) - z_high.astype(jnp.float32)).astype(jnp.bfloat16)
+
+    *received, z_rates = pl.pallas_call(
         functools.partial(exchange_kernel, sizes),
-        out_shape=(plane,) * 4 + (edge,) * 2,
+        out_shape=(plane,) * 4 + (edge,) * 2
+        + (jax.ShapeDtypeStruct((3, cells, width, depth), jnp.float32),),
         in_specs=[
-            pl.BlockSpec(memory_space=SMEM),
             pl.BlockSpec(memory_space=SMEM),
             pl.BlockSpec(memory_space=pl.ANY),
             pl.BlockSpec(memory_space=pl.ANY),
+            pl.BlockSpec(memory_space=VMEM),
+            pl.BlockSpec(memory_space=VMEM),
         ],
-        out_specs=(pl.BlockSpec(memory_space=VMEM),) * 6,
-        scratch_shapes=[VMEM((5, cells, width, depth), jnp.float32)]
+        out_specs=(pl.BlockSpec(memory_space=VMEM),) * 6 + (pl.BlockSpec(memory_space=pl.ANY),),
+        scratch_shapes=[VMEM((3, cells, width, depth), jnp.float32)]
+        + [VMEM((5, cells, width, depth), jnp.float32)]
         + [scratch_plane] * 6
         + [
             pltpu.SemaphoreType.DMA((5,)),
+            pltpu.SemaphoreType.DMA((3,)),
             pltpu.SemaphoreType.DMA((8, 5)),
             pltpu.SemaphoreType.DMA((8, 5)),
         ],
         compiler_params=pltpu.CompilerParams(
-            collective_id=0, has_side_effects=True, vmem_limit_bytes=40 * 1024 * 1024
+            collective_id=0, has_side_effects=True, vmem_limit_bytes=60 * 1024 * 1024
         ),
-    )(mine(weights), mine(links), state, mean_flow)
-
-    operator = dense_derivative(depth).T.astype(np.float32)
-    z_high = jnp.asarray(operator).astype(jnp.bfloat16)
-    z_low = (jnp.asarray(operator) - z_high.astype(jnp.float32)).astype(jnp.bfloat16)
+    )(table, state, mean_flow, z_high, z_low)
 
     planes = width * groups
     along_x = face_cell // (planes * depth) - block * cells
     along_y = face_cell // depth % planes - group * width
     along_z = face_cell % depth
     row = (along_x * width + along_y).reshape(1, faces)
+
+    geometry = jnp.concatenate(
+        [face_normal, face_pos, along_z.astype(jnp.float32)[None]]
+    ).T
 
     def whole(*shape):
         return pl.BlockSpec(shape, lambda j: (0,) * len(shape))
@@ -482,12 +508,12 @@
             jax.ShapeDtypeStruct((BINS, observers), jnp.float32),
         ),
         in_specs=[
-            smem, smem, smem,
+            smem, smem,
             whole(4, cells, width, depth), whole(cells, width, depth),
             plane_spec, plane_spec, plane_spec, plane_spec,
             whole(3, cells, TILE, depth), whole(3, cells, TILE, depth),
-            whole(depth, depth), whole(depth, depth),
-            whole(faces, 1), whole(faces, 3), whole(faces, 3),
+            pl.BlockSpec((3, cells, TILE, depth), lambda j: (0, 0, j, 0)),
+            whole(faces, 7),
             whole(3, observers), whole(faces, observers),
         ],
         out_specs=(
@@ -497,15 +523,14 @@
         scratch_shapes=[
             VMEM((3, cells, width + 2 * TILE, depth), jnp.float32),
             VMEM((5, cells, TILE, depth), jnp.float32),
-            VMEM((3, cells, TILE, depth), jnp.float32),
             VMEM((5, cells * width, depth), jnp.float32),
             VMEM((5, faces, depth), jnp.float32),
         ],
         compiler_params=pltpu.CompilerParams(**params),
     )(
-        row, mine(sweep), mine(edges.reshape(blocks, 1, -1)),
+        row, table,
         state, mean_flow, *received,
-        z_high, z_low, along_z.reshape(faces, 1), face_normal.T, face_pos.T,
+        z_rates, geometry,
         observer_pos, time_bin,
     )
     devices = blocks * groups

time: 90.9 us -> 75.5 us (0.83)
  local copies, waits for them, and re-layouts: 19.3 us -> 5.04 us
  Pallas kernels: 68.8 us -> 66.9 us
    unnamed x19 -> x1, local copies, waits for them, and re-layouts: 13 us -> 1.3 us
    pallas_call x1, Pallas kernels: 26.3 us -> 23.1 us  [per_device(): pl.pallas_call(functools.partial(main_kernel, cells, width, depth), grid=...]
    squeeze x4 -> x1, local copies, waits for them, and re-layouts: 3.85 us -> 1.26 us  [per_device(): lax.dynamic_index_in_dim(jnp.asarray(tables), block, 0, keepdims=False)]
    pallas_call x1, Pallas kernels: 32.2 us -> 33.5 us  [per_device(): pl.pallas_call(functools.partial(exchange_kernel, sizes), out_shape=(plan...]
    convert_element_type x0 -> x1, other arithmetic: none -> 1.26 us  [per_device(): along_z.astype(jnp.float32)[None]]
    select_n x1 -> x0, other arithmetic: 1.24 us -> none  [per_device(): along_z = face_cell % depth]
where the time goes in v3:
time: 75.5 us; the launch traced here: 74.6 us
  Pallas kernels  66.9 us (89%)
  local copies, waits for them, and re-layouts  5.04 us (7%)
  other arithmetic  1.99 us (3%)
    pallas_call x1, Pallas kernels, per_device(): pl.pallas_call(functools.partial(exchange_kernel, sizes), out_shape=(plan...  33.5 us
    pallas_call x1, Pallas kernels, per_device(): pl.pallas_call(functools.partial(main_kernel, cells, width, depth), grid=...  23.1 us
    pallas_call x1, Pallas kernels, per_device(): pl.pallas_call(functools.partial(signal_kernel, groups, devices), out_sha...  10.2 us
    transpose x1, local copies, waits for them, and re-layouts, per_device(): signal.T.reshape(devices, share, BINS)  1.72 us

profile of v3, /device:TPU:0, one launch (start us, length us, event | category | flops | bytes accessed | tf_op | source)
XLA Modules:
  0.0 74.6 jit_solution(16315822868013037351)
XLA Ops:
  0.6 1.3 %dynamic-slice_bitcast_fusion.table_ref = f32[1,188]{1,0:T(1,128)} fusion(f32[8,1,188]{2,1,0:T(1,128)} %constant.64.clone, s32[]{:T(128)S(6)} %select_n.26), kind=kLoop, calls=%fused_computation.11 | loop fusion | bytes 1508 | tf_op jit(solution)/shard_map/jit(dynamic_index_in_dim)/squeeze | solution.py:454
  1.9 1.3 %fusion.2 = (f32[192]{0:T(256)S(1)}, s32[192]{0:T(256)}) fusion(s32[192]{0:T(256)} %param.11, s32[]{:T(128)S(6)} %mul.15, s32[]{:T(128)S(6)} %mul.12), kind=kLoop, calls=%fused_computation.10 | loop fusion | flops 6912 | bytes 2312 | tf_op jit(solution)/shard_map/convert_element_type | solution.py:496
  3.2 0.7 pad_maximum_fusion
  3.9 0.8 %copy.18 = f32[7,192]{0,1:T(8,128)} copy(f32[7,192]{1,0:T(8,128)S(1)} %pad_maximum_fusion) | data formatting | bytes 10752 | tf_op jit(solution)/shard_map/concatenate | solution.py:495
  4.6 33.5 %shard_map.104 = (f32[5,48,256]{2,1,0:T(8,128)}, f32[5,48,256]{2,1,0:T(8,128)}, f32[5,48,256]{2,1,0:T(8,128)}, f32[5,48,256]{2,1,0:T(8,128)}, f32[3,32,8,256]{3,...) custom-call(f32[1,188]{1,0:T(1,128)} %dynamic-slice_bitcast_fusion.table_ref, ...), custom_call_target="tpu_custom_call" | custom-call | tf_op jit(solution)/shard_map/pallas_call | solution.py:463
  38.2 23.1 %shard_map.105 = (f32[4,32,48,256]{3,2,1,0:T(8,128)}, f32[64,512]{1,0:T(8,128)}) custom-call(s32[1,192]{1,0:T(1,128)} %bitcast.11, f32[1,188]{1,0:T(1,128)} %dynamic-slice_bitcast_fusion.table_ref, f32[4,32,48,256]{3,2,1,0:T(8,128)} %state_ref.3, f32[32,48,256]{2,1,0:T(8,128)} %flow_ref.3, f32[5,48,256]{2,1,0:T(8,128)} %get-tuple-element.11.left_sum, ...), custom_call_target="tpu_custom_call" | custom-call | tf_op jit(solution)/shard_map/pallas_call | solution.py:503
  61.3 1.7 %copy.19 = f32[512,64]{1,0:T(8,128)} copy(f32[512,64]{0,1:T(8,128)} %bitcast.9) | data formatting | bytes 262144 | tf_op jit(solution)/shard_map/transpose | solution.py:549
  63.1 10.2 %shard_map.106 = f32[16,64]{1,0:T(8,128)} custom-call(f32[32,16,64]{2,1,0:T(8,128)} %bitcast.7), custom_call_target="tpu_custom_call" | custom-call | tf_op jit(solution)/shard_map/pallas_call | solution.py:538
  73.3 1.3 %copy.21 = f32[16,64]{1,0:T(8,128)} copy(f32[16,64]{1,0:T(8,128)} %shard_map.106) | data formatting | bytes 8192
